TPU v7x, 128 devices: a whole 4x4x4 slice. The times are simulated.
128 devices in a mesh: tm: 8 (over x, core), lat: 4 (over y), lon: 4 (over z).
Axes of the slice: x: 4, y: 4, z: 4, core: 2. Of those that a mesh axis runs over, the one named last changes fastest.
Arguments:
- forcing: float32 [32, 512, 2048], P('tm', 'lat', 'lon'), may hold values from -17 to 17
- depth: float32 [512, 2048], P('lat', 'lon'), may hold values from 0.2 to 2
- mask: int32 [512, 2048], P('lat', 'lon'), may hold values 0 or 1
- guess: float32 [8, 512, 2048], P('tm', 'lat', 'lon'), may hold values from -6 to 6
Outputs:
- adjoint: float32 [32, 512, 2048], P('tm', 'lat', 'lon')
All inputs are finite; a program needn't handle non-finite values. No bound on the sum of `mask` on one device may be relied on, other than what follows from the above.
Results may differ from a plain program's by a relative error of at most 0.0001.
Values sent between devices are 32-bit elements; how exact they have to be, the bound alone decides.
A program may use at most 64 MiB of HBM per device.

v0:
```python
import jax
import jax.numpy as jnp
from jax import lax
from jax.sharding import PartitionSpec as P

FS = 4
FINE_ITERS = 2


COUPLING = 3.0
EPSILON = 1e-06


def with_halo(block, sides, width):
    for axis, dim in sides:
        count = lax.axis_size(axis)
        forward = [(i, i + 1) for i in range(count - 1)]
        forward.append((count - 1, 0))
        backward = [(target, source) for source, target in forward]
        low = lax.ppermute(
            lax.slice_in_dim(block, block.shape[dim] - width, None, axis=dim), axis, forward
        )
        high = lax.ppermute(lax.slice_in_dim(block, 0, width, axis=dim), axis, backward)
        block = jnp.concatenate([low, block, high], axis=dim)
    return block


def extended(array, sides, width):
    edges = {}
    for axis, dim in sides:
        size, length = (lax.axis_size(axis), array.shape[dim])
        up = [(i, (i + 1) % size) for i in range(size)]
        last = lax.slice_in_dim(array, length - width, length, axis=dim)
        initial = lax.slice_in_dim(array, 0, width, axis=dim)
        edges[dim] = (
            lax.ppermute(last, axis, up),
            lax.ppermute(initial, axis, [(b, a) for a, b in up]),
        )
    done = []
    for _, dim in sides:
        low, high = edges[dim]
        around = [(width, width) if d in done else (0, 0) for d in range(array.ndim)]
        array = jnp.concatenate([jnp.pad(low, around), array, jnp.pad(high, around)], axis=dim)
        done.append(dim)
    return array


def copy_for_each(array, axis):
    size = lax.axis_size(axis)
    return lax.all_to_all(
        jnp.broadcast_to(array[None], (size, *array.shape)), axis, 0, 0, tiled=True
    )


def over_copies(array, axis):
    return copy_for_each(array, axis).sum(axis=0)


def together(arrays, axis):
    ends = [0]
    for a in arrays:
        ends.append(ends[-1] + a.size)
    so_far = over_copies(jnp.concatenate([a.ravel() for a in arrays]), axis)
    return tuple((so_far[b:e].reshape(a.shape) for a, b, e in zip(arrays, ends, ends[1:])))


def shifted(array, axis, by):
    size = lax.axis_size(axis)
    pairs = [(i, i + by) for i in range(size) if 0 <= i + by < size]
    return lax.ppermute(array, axis, pairs)


def face_terms(depth, mask):
    wet = mask.astype(jnp.float32)
    stacked = jnp.stack([wet, depth])
    padded = with_halo(stacked, (("lat", 1), ("lon", 2)), 1)
    rows = depth.shape[0]
    wet_pad = padded[0]
    deep_pad = padded[1]
    middle_wet = wet_pad[1:-1]
    middle_deep = deep_pad[1:-1]
    across = (
        COUPLING
        * middle_wet[:, :-1]
        * middle_wet[:, 1:]
        * 0.5
        * (middle_deep[:, :-1] + middle_deep[:, 1:])
    )
    along = (
        COUPLING
        * wet_pad[:-1, 1:-1]
        * wet_pad[1:, 1:-1]
        * 0.5
        * (deep_pad[:-1, 1:-1] + deep_pad[1:, 1:-1])
    )
    first = lax.axis_index("lat") == 0
    final = lax.axis_index("lat") == lax.axis_size("lat") - 1
    face_row = lax.broadcasted_iota(jnp.int32, along.shape, 0)
    along = jnp.where(first & (face_row == 0) | final & (face_row == rows), 0.0, along)
    return (across[:, 1:], across[:, :-1], along[1:], along[:-1])


def apply_op(field, faces, factor):
    east, west, north, south = faces
    padded = extended(field, (("lat", 0), ("lon", 1)), 1)
    spread = east * (field - padded[1:-1, 2:]) + west * (field - padded[1:-1, :-2])
    spread = spread + north * (field - padded[2:, 1:-1]) + south * (field - padded[:-2, 1:-1])
    return field + factor * spread


def paired(residual, image):
    return together((jnp.sum(residual * residual), jnp.sum(residual * image)), ("lat", "lon"))


def fine_solve(source, faces):
    solution = jnp.zeros_like(source)
    residual = source
    direction = source
    image = apply_op(source, faces, 1.0)
    norm_now, product = paired(source, image)
    alpha = norm_now / (product + EPSILON)
    along = image
    for level in range(FINE_ITERS):
        solution = solution + alpha * direction
        residual = residual - alpha * along
        if level + 1 < FINE_ITERS:
            image = apply_op(residual, faces, 1.0)
            norm_next, product = paired(residual, image)
            ratio = norm_next / (norm_now + EPSILON)
            alpha = norm_next / (product - ratio * norm_next / alpha + EPSILON)
            direction = residual + ratio * direction
            along = image + ratio * along
            norm_now = norm_next
    return solution


def coarse_solve(source, faces):
    image = apply_op(source, faces, float(FS))
    norm_now, product = together(
        (jnp.sum(source * source), jnp.sum(source * image)), ("lat", "lon")
    )
    return norm_now / (product + EPSILON) * source


def local(forcing, depth, mask, guess):
    faces = face_terms(depth, mask)
    start = guess[0]
    value = start
    for level in range(FS - 1, 0, -1):
        value = fine_solve(value, faces) + forcing[level]
    finished = fine_solve(value, faces) + forcing[0]
    offset = finished - coarse_solve(start, faces)
    position = lax.axis_index("tm")
    slab_count = lax.axis_size("tm")
    is_final = position == slab_count - 1

    def turn(index, upper):
        here = coarse_solve(upper, faces) + offset
        moved = shifted(here, "tm", -1)
        return jnp.where(is_final, start, moved)

    upper = lax.fori_loop(0, slab_count - 1, turn, start)
    here = coarse_solve(upper, faces) + offset
    value = upper
    later = []
    for level in range(FS - 1, 0, -1):
        value = fine_solve(value, faces) + forcing[level]
        later.append(value)
    return jnp.stack([here] + later[::-1])


def solution(mesh):
    return jax.shard_map(
        local,
        mesh=mesh,
        in_specs=(P("tm", "lat", "lon"), P("lat", "lon"), P("lat", "lon"), P("tm", "lat", "lon")),
        out_specs=P("tm", "lat", "lon"),
        check_vma=False,
    )
```

profile of v0, /device:TPU:2, one launch (start us, length us, event | category | flops | bytes accessed | tf_op | source)
XLA Modules:
  0.0 633.3 jit_solution(323414678042733607)
XLA Ops:
  4.4 4.1 collective-permute-start.11
  22.9 10.1 %all_to_all.106 = f32[16,1,2]{2,1,0:T(1,128)S(1)} all-to-all(f32[16,1,2]{2,1,0:T(1,128)S(1)} %broadcast_in_dim.39), channel_id=1, replica_groups=mesh['tm'=8,'lat'=4,'lon'=4] {'lat','lon'}, dimensions={0} | all-to-all | bytes 256 | tf_op jit(solution)/shard_map/all_to_all | solution.py:50
  51.9 6.8 %all-to-all-done.2 = f32[16,1,2]{2,1,0:T(1,128)S(1)} async-done(((f32[16,1,2]{2,1,0:T(1,128)}), f32[16,1,2]{2,1,0:T(1,128)S(1)}, u32[]{:S(2)}, u32[]{:S(2)}) %all-to-all-start.2) | async-done | bytes 160 | tf_op jit(solution)/shard_map/all_to_all | solution.py:50
  74.9 10.1 %all_to_all.107 = f32[16,1,2]{2,1,0:T(1,128)S(1)} all-to-all(f32[16,1,2]{2,1,0:T(1,128)S(1)} %broadcast_in_dim.41), channel_id=1, replica_groups=mesh['tm'=8,'lat'=4,'lon'=4] {'lat','lon'}, dimensions={0} | all-to-all | bytes 256 | tf_op jit(solution)/shard_map/all_to_all | solution.py:50
  103.9 6.8 %all-to-all-done.4 = f32[16,1,2]{2,1,0:T(1,128)S(1)} async-done(((f32[16,1,2]{2,1,0:T(1,128)}), f32[16,1,2]{2,1,0:T(1,128)S(1)}, u32[]{:S(2)}, u32[]{:S(2)}) %all-to-all-start.4) | async-done | bytes 160 | tf_op jit(solution)/shard_map/all_to_all | solution.py:50
  127.1 10.1 %all_to_all.108 = f32[16,1,2]{2,1,0:T(1,128)S(1)} all-to-all(f32[16,1,2]{2,1,0:T(1,128)S(1)} %broadcast_in_dim.47), channel_id=1, replica_groups=mesh['tm'=8,'lat'=4,'lon'=4] {'lat','lon'}, dimensions={0} | all-to-all | bytes 256 | tf_op jit(solution)/shard_map/all_to_all | solution.py:50
  156.1 6.8 %all-to-all-done.6 = f32[16,1,2]{2,1,0:T(1,128)S(1)} async-done(((f32[16,1,2]{2,1,0:T(1,128)}), f32[16,1,2]{2,1,0:T(1,128)S(1)}, u32[]{:S(2)}, u32[]{:S(2)}) %all-to-all-start.6) | async-done | bytes 160 | tf_op jit(solution)/shard_map/all_to_all | solution.py:50
  175.1 6.4 %all-to-all-start.9 = ((f32[16,1,2]{2,1,0:T(1,128)}), f32[16,1,2]{2,1,0:T(1,128)S(1)}, u32[]{:S(2)}, u32[]{:S(2)}) async-start(f32[16,1,2]{2,1,0:T(1,128)} %broadcast_in_dim.51), calls=%async_computation.9 | async-start | bytes 16384 | tf_op jit(solution)/shard_map/all_to_all | solution.py:50
  182.9 6.2 all-to-all-done.9
  193.2 7.4 %all-to-all-done.7 = f32[16,1,2]{2,1,0:T(1,128)S(1)} async-done(((f32[16,1,2]{2,1,0:T(1,128)}), f32[16,1,2]{2,1,0:T(1,128)S(1)}, u32[]{:S(2)}, u32[]{:S(2)}) %all-to-all-start.7) | async-done | bytes 160 | tf_op jit(solution)/shard_map/all_to_all | solution.py:50
  212.3 6.4 %all-to-all-start.8 = ((f32[16,1,2]{2,1,0:T(1,128)}), f32[16,1,2]{2,1,0:T(1,128)S(1)}, u32[]{:S(2)}, u32[]{:S(2)}) async-start(f32[16,1,2]{2,1,0:T(1,128)} %broadcast_in_dim.50), calls=%async_computation.8 | async-start | bytes 16384 | tf_op jit(solution)/shard_map/all_to_all | solution.py:50
  220.1 6.2 all-to-all-done.8
  231.3 220.6 %while.12 = (s32[]{:T(128)}, f32[128,512]{1,0:T(8,128)S(1)}, pred[]{:T(512)}, f32[128,512]{1,0:T(8,128)S(1)}, f32[128,512]{1,0:T(8,128)S(1)}, /*index=5*/f32[128...) while((s32[]{:T(128)}, f32[128,512]{1,0:T(8,128)S(1)}, ...), condition=%wide.region_30.31_spmd, body=%wide.region_26.0_spmd.sunk | while | flops 2228258 | bytes 3968926 | solution.py:162
  242.4 12.0 %all_to_all.111 = f32[16,1,2]{2,1,0:T(1,128)S(1)} all-to-all(f32[16,1,2]{2,1,0:T(1,128)S(1)} %broadcast_in_dim.61), channel_id=1, replica_groups=mesh['tm'=8,'lat'=4,'lon'=4] {'lat','lon'}, dimensions={0} | all-to-all | bytes 256 | tf_op jit(solution)/shard_map/while/body/eval_jaxpr/all_to_all | solution.py:50
  258.2 3.9 collective-permute-done.4
  274.3 12.2 %all_to_all.111 = f32[16,1,2]{2,1,0:T(1,128)S(1)} all-to-all(f32[16,1,2]{2,1,0:T(1,128)S(1)} %broadcast_in_dim.61), channel_id=1, replica_groups=mesh['tm'=8,'lat'=4,'lon'=4] {'lat','lon'}, dimensions={0} | all-to-all | bytes 256 | tf_op jit(solution)/shard_map/while/body/eval_jaxpr/all_to_all | solution.py:50
  290.3 3.9 collective-permute-done.4
  306.5 11.7 %all_to_all.111 = f32[16,1,2]{2,1,0:T(1,128)S(1)} all-to-all(f32[16,1,2]{2,1,0:T(1,128)S(1)} %broadcast_in_dim.61), channel_id=1, replica_groups=mesh['tm'=8,'lat'=4,'lon'=4] {'lat','lon'}, dimensions={0} | all-to-all | bytes 256 | tf_op jit(solution)/shard_map/while/body/eval_jaxpr/all_to_all | solution.py:50
  322.0 3.9 collective-permute-done.4
  337.8 11.7 %all_to_all.111 = f32[16,1,2]{2,1,0:T(1,128)S(1)} all-to-all(f32[16,1,2]{2,1,0:T(1,128)S(1)} %broadcast_in_dim.61), channel_id=1, replica_groups=mesh['tm'=8,'lat'=4,'lon'=4] {'lat','lon'}, dimensions={0} | all-to-all | bytes 256 | tf_op jit(solution)/shard_map/while/body/eval_jaxpr/all_to_all | solution.py:50
  353.3 3.9 collective-permute-done.4
  369.2 11.7 %all_to_all.111 = f32[16,1,2]{2,1,0:T(1,128)S(1)} all-to-all(f32[16,1,2]{2,1,0:T(1,128)S(1)} %broadcast_in_dim.61), channel_id=1, replica_groups=mesh['tm'=8,'lat'=4,'lon'=4] {'lat','lon'}, dimensions={0} | all-to-all | bytes 256 | tf_op jit(solution)/shard_map/while/body/eval_jaxpr/all_to_all | solution.py:50
  400.5 11.7 %all_to_all.111 = f32[16,1,2]{2,1,0:T(1,128)S(1)} all-to-all(f32[16,1,2]{2,1,0:T(1,128)S(1)} %broadcast_in_dim.61), channel_id=1, replica_groups=mesh['tm'=8,'lat'=4,'lon'=4] {'lat','lon'}, dimensions={0} | all-to-all | bytes 256 | tf_op jit(solution)/shard_map/while/body/eval_jaxpr/all_to_all | solution.py:50
  431.9 11.7 %all_to_all.111 = f32[16,1,2]{2,1,0:T(1,128)S(1)} all-to-all(f32[16,1,2]{2,1,0:T(1,128)S(1)} %broadcast_in_dim.61), channel_id=1, replica_groups=mesh['tm'=8,'lat'=4,'lon'=4] {'lat','lon'}, dimensions={0} | all-to-all | bytes 256 | tf_op jit(solution)/shard_map/while/body/eval_jaxpr/all_to_all | solution.py:50
  452.0 10.1 %collective-permute-start.41 = (f32[1,512]{1,0:T(1,128)S(1)}, f32[1,512]{1,0:T(1,128)S(1)}, u32[]{:S(2)}, u32[]{:S(2)}) collective-permute-start(f32[1,512]{1,0:T(1,128)S(1)} %get-tuple-element.267), channel_id=1, source_target_pairs={{0,4},{4,8},{8,12},{12,0},{1,5},{5,9},{9,13},{13,1},{2,6},{6,10},{... | collective-permute-start | bytes 6152 | tf_op jit(solution)/shard_map/ppermute | solution.py:36
  479.1 6.2 all-to-all-done.11
  490.7 6.2 all-to-all-done.10
  516.6 6.8 %all-to-all-done.12 = f32[16,1,2]{2,1,0:T(1,128)S(1)} async-done(((f32[16,1,2]{2,1,0:T(1,128)}), f32[16,1,2]{2,1,0:T(1,128)S(1)}, u32[]{:S(2)}, u32[]{:S(2)}) %all-to-all-start.12) | async-done | bytes 160 | tf_op jit(solution)/shard_map/all_to_all | solution.py:50
  539.7 10.1 %all_to_all.109 = f32[16,1,2]{2,1,0:T(1,128)S(1)} all-to-all(f32[16,1,2]{2,1,0:T(1,128)S(1)} %broadcast_in_dim.55), channel_id=1, replica_groups=mesh['tm'=8,'lat'=4,'lon'=4] {'lat','lon'}, dimensions={0} | all-to-all | bytes 256 | tf_op jit(solution)/shard_map/all_to_all | solution.py:50
  568.9 6.8 %all-to-all-done.14 = f32[16,1,2]{2,1,0:T(1,128)S(1)} async-done(((f32[16,1,2]{2,1,0:T(1,128)}), f32[16,1,2]{2,1,0:T(1,128)S(1)}, u32[]{:S(2)}, u32[]{:S(2)}) %all-to-all-start.14) | async-done | bytes 160 | tf_op jit(solution)/shard_map/all_to_all | solution.py:50
  592.1 10.1 %all_to_all.110 = f32[16,1,2]{2,1,0:T(1,128)S(1)} all-to-all(f32[16,1,2]{2,1,0:T(1,128)S(1)} %broadcast_in_dim.57), channel_id=1, replica_groups=mesh['tm'=8,'lat'=4,'lon'=4] {'lat','lon'}, dimensions={0} | all-to-all | bytes 256 | tf_op jit(solution)/shard_map/all_to_all | solution.py:50
  621.2 6.8 %all-to-all-done.16 = f32[16,1,2]{2,1,0:T(1,128)S(1)} async-done(((f32[16,1,2]{2,1,0:T(1,128)}), f32[16,1,2]{2,1,0:T(1,128)S(1)}, u32[]{:S(2)}, u32[]{:S(2)}) %all-to-all-start.16) | async-done | bytes 160 | tf_op jit(solution)/shard_map/all_to_all | solution.py:50
  (395 shorter events, 336.8 us)
Async XLA Ops:
  4.4 12.7 %collective-permute-start.11 = (f32[128,1]{1,0:T(8,128)S(1)}, f32[128,1]{1,0:T(8,128)S(1)}, u32[]{:S(2)}, u32[]{:S(2)}) collective-permute-start(f32[128,1]{1,0:T(8,128)S(1)} %get-tuple-element.296), channel_id=1, source_target_pairs={{1,0},{2,1},{3,2},{0,3},{5,4},{6,5},{7,6},{4,7},{9,8},{10,9},{11,1... | collective-permute-start | bytes 1544 | tf_op jit(solution)/shard_map/ppermute | solution.py:37
  35.0 10.1 %collective-permute-start.13 = (f32[1,512]{1,0:T(1,128)S(1)}, f32[1,512]{1,0:T(1,128)S(1)}, u32[]{:S(2)}, u32[]{:S(2)}) collective-permute-start(f32[1,512]{1,0:T(1,128)S(1)} %get-tuple-element.295), channel_id=1, source_target_pairs={{0,4},{4,8},{8,12},{12,0},{1,5},{5,9},{9,13},{13,1},{2,6},{6,10},{... | collective-permute-start | bytes 6152 | tf_op jit(solution)/shard_map/ppermute | solution.py:36
  35.6 9.5 %collective-permute-start.14 = (f32[1,512]{1,0:T(1,128)S(1)}, f32[1,512]{1,0:T(1,128)S(1)}, u32[]{:S(2)}, u32[]{:S(2)}) collective-permute-start(f32[1,512]{1,0:T(1,128)S(1)} %get-tuple-element.294), channel_id=1, source_target_pairs={{4,0},{8,4},{12,8},{0,12},{5,1},{9,5},{13,9},{1,13},{6,2},{10,6},{... | collective-permute-start | bytes 6152 | tf_op jit(solution)/shard_map/ppermute | solution.py:37
  47.8 10.9 %all-to-all-start.2 = ((f32[16,1,2]{2,1,0:T(1,128)}), f32[16,1,2]{2,1,0:T(1,128)S(1)}, u32[]{:S(2)}, u32[]{:S(2)}) async-start(f32[16,1,2]{2,1,0:T(1,128)} %broadcast_in_dim.40), calls=%async_computation.2 | async-start | bytes 16384 | tf_op jit(solution)/shard_map/all_to_all | solution.py:50
  62.5 10.1 %collective-permute-start.17 = (f32[1,512]{1,0:T(1,128)S(1)}, f32[1,512]{1,0:T(1,128)S(1)}, u32[]{:S(2)}, u32[]{:S(2)}) collective-permute-start(f32[1,512]{1,0:T(1,128)S(1)} %get-tuple-element.291), channel_id=1, source_target_pairs={{0,4},{4,8},{8,12},{12,0},{1,5},{5,9},{9,13},{13,1},{2,6},{6,10},{... | collective-permute-start | bytes 6152 | tf_op jit(solution)/shard_map/ppermute | solution.py:36
  63.1 9.4 %collective-permute-start.18 = (f32[1,512]{1,0:T(1,128)S(1)}, f32[1,512]{1,0:T(1,128)S(1)}, u32[]{:S(2)}, u32[]{:S(2)}) collective-permute-start(f32[1,512]{1,0:T(1,128)S(1)} %get-tuple-element.290), channel_id=1, source_target_pairs={{4,0},{8,4},{12,8},{0,12},{5,1},{9,5},{13,9},{1,13},{6,2},{10,6},{... | collective-permute-start | bytes 6152 | tf_op jit(solution)/shard_map/ppermute | solution.py:37
  87.0 10.1 %collective-permute-start.21 = (f32[1,512]{1,0:T(1,128)S(1)}, f32[1,512]{1,0:T(1,128)S(1)}, u32[]{:S(2)}, u32[]{:S(2)}) collective-permute-start(f32[1,512]{1,0:T(1,128)S(1)} %get-tuple-element.287), channel_id=1, source_target_pairs={{0,4},{4,8},{8,12},{12,0},{1,5},{5,9},{9,13},{13,1},{2,6},{6,10},{... | collective-permute-start | bytes 6152 | tf_op jit(solution)/shard_map/ppermute | solution.py:36
  87.6 9.4 %collective-permute-start.22 = (f32[1,512]{1,0:T(1,128)S(1)}, f32[1,512]{1,0:T(1,128)S(1)}, u32[]{:S(2)}, u32[]{:S(2)}) collective-permute-start(f32[1,512]{1,0:T(1,128)S(1)} %get-tuple-element.286), channel_id=1, source_target_pairs={{4,0},{8,4},{12,8},{0,12},{5,1},{9,5},{13,9},{1,13},{6,2},{10,6},{... | collective-permute-start | bytes 6152 | tf_op jit(solution)/shard_map/ppermute | solution.py:37
  99.8 10.9 %all-to-all-start.4 = ((f32[16,1,2]{2,1,0:T(1,128)}), f32[16,1,2]{2,1,0:T(1,128)S(1)}, u32[]{:S(2)}, u32[]{:S(2)}) async-start(f32[16,1,2]{2,1,0:T(1,128)} %broadcast_in_dim.46), calls=%async_computation.4 | async-start | bytes 16384 | tf_op jit(solution)/shard_map/all_to_all | solution.py:50
  114.4 10.3 %collective-permute-start.25 = (f32[1,512]{1,0:T(1,128)S(1)}, f32[1,512]{1,0:T(1,128)S(1)}, u32[]{:S(2)}, u32[]{:S(2)}) collective-permute-start(f32[1,512]{1,0:T(1,128)S(1)} %get-tuple-element.283), channel_id=1, source_target_pairs={{0,4},{4,8},{8,12},{12,0},{1,5},{5,9},{9,13},{13,1},{2,6},{6,10},{... | collective-permute-start | bytes 6152 | tf_op jit(solution)/shard_map/ppermute | solution.py:36
  115.3 9.4 %collective-permute-start.26 = (f32[1,512]{1,0:T(1,128)S(1)}, f32[1,512]{1,0:T(1,128)S(1)}, u32[]{:S(2)}, u32[]{:S(2)}) collective-permute-start(f32[1,512]{1,0:T(1,128)S(1)} %get-tuple-element.282), channel_id=1, source_target_pairs={{4,0},{8,4},{12,8},{0,12},{5,1},{9,5},{13,9},{1,13},{6,2},{10,6},{... | collective-permute-start | bytes 6152 | tf_op jit(solution)/shard_map/ppermute | solution.py:37
  139.1 10.1 %collective-permute-start.29 = (f32[1,512]{1,0:T(1,128)S(1)}, f32[1,512]{1,0:T(1,128)S(1)}, u32[]{:S(2)}, u32[]{:S(2)}) collective-permute-start(f32[1,512]{1,0:T(1,128)S(1)} %get-tuple-element.279), channel_id=1, source_target_pairs={{0,4},{4,8},{8,12},{12,0},{1,5},{5,9},{9,13},{13,1},{2,6},{6,10},{... | collective-permute-start | bytes 6152 | tf_op jit(solution)/shard_map/ppermute | solution.py:36
  139.8 9.4 %collective-permute-start.30 = (f32[1,512]{1,0:T(1,128)S(1)}, f32[1,512]{1,0:T(1,128)S(1)}, u32[]{:S(2)}, u32[]{:S(2)}) collective-permute-start(f32[1,512]{1,0:T(1,128)S(1)} %get-tuple-element.278), channel_id=1, source_target_pairs={{4,0},{8,4},{12,8},{0,12},{5,1},{9,5},{13,9},{1,13},{6,2},{10,6},{... | collective-permute-start | bytes 6152 | tf_op jit(solution)/shard_map/ppermute | solution.py:37
  152.0 10.9 %all-to-all-start.6 = ((f32[16,1,2]{2,1,0:T(1,128)}), f32[16,1,2]{2,1,0:T(1,128)S(1)}, u32[]{:S(2)}, u32[]{:S(2)}) async-start(f32[16,1,2]{2,1,0:T(1,128)} %broadcast_in_dim.48), calls=%async_computation.6 | async-start | bytes 16384 | tf_op jit(solution)/shard_map/all_to_all | solution.py:50
  175.1 14.0 %all-to-all-start.9 = ((f32[16,1,2]{2,1,0:T(1,128)}), f32[16,1,2]{2,1,0:T(1,128)S(1)}, u32[]{:S(2)}, u32[]{:S(2)}) async-start(f32[16,1,2]{2,1,0:T(1,128)} %broadcast_in_dim.51), calls=%async_computation.9 | async-start | bytes 16384 | tf_op jit(solution)/shard_map/all_to_all | solution.py:50
  189.7 10.9 %all-to-all-start.7 = ((f32[16,1,2]{2,1,0:T(1,128)}), f32[16,1,2]{2,1,0:T(1,128)S(1)}, u32[]{:S(2)}, u32[]{:S(2)}) async-start(f32[16,1,2]{2,1,0:T(1,128)} %broadcast_in_dim.49), calls=%async_computation.7 | async-start | bytes 16384 | tf_op jit(solution)/shard_map/all_to_all | solution.py:50
  212.3 14.0 %all-to-all-start.8 = ((f32[16,1,2]{2,1,0:T(1,128)}), f32[16,1,2]{2,1,0:T(1,128)S(1)}, u32[]{:S(2)}, u32[]{:S(2)}) async-start(f32[16,1,2]{2,1,0:T(1,128)} %broadcast_in_dim.50), calls=%async_computation.8 | async-start | bytes 16384 | tf_op jit(solution)/shard_map/all_to_all | solution.py:50
  294.8 9.5 %collective-permute-start = (f32[1,512]{1,0:T(1,128)S(1)}, f32[1,512]{1,0:T(1,128)S(1)}, u32[]{:S(2)}, u32[]{:S(2)}) collective-permute-start(f32[1,512]{1,0:T(1,128)S(1)} %get-tuple-element.401), channel_id=1, source_target_pairs={{0,4},{4,8},{8,12},{12,0},{1,5},{5,9},{9,13},{13,1},{2,6},{6,10},{... | collective-permute-start | bytes 6152 | tf_op jit(solution)/shard_map/while/body/eval_jaxpr/ppermute | solution.py:36
  452.0 19.6 %collective-permute-start.41 = (f32[1,512]{1,0:T(1,128)S(1)}, f32[1,512]{1,0:T(1,128)S(1)}, u32[]{:S(2)}, u32[]{:S(2)}) collective-permute-start(f32[1,512]{1,0:T(1,128)S(1)} %get-tuple-element.267), channel_id=1, source_target_pairs={{0,4},{4,8},{8,12},{12,0},{1,5},{5,9},{9,13},{13,1},{2,6},{6,10},{... | collective-permute-start | bytes 6152 | tf_op jit(solution)/shard_map/ppermute | solution.py:36
  462.1 9.5 %collective-permute-start.42 = (f32[1,512]{1,0:T(1,128)S(1)}, f32[1,512]{1,0:T(1,128)S(1)}, u32[]{:S(2)}, u32[]{:S(2)}) collective-permute-start(f32[1,512]{1,0:T(1,128)S(1)} %get-tuple-element.266), channel_id=1, source_target_pairs={{4,0},{8,4},{12,8},{0,12},{5,1},{9,5},{13,9},{1,13},{6,2},{10,6},{... | collective-permute-start | bytes 6152 | tf_op jit(solution)/shard_map/ppermute | solution.py:37
  474.4 10.9 %all-to-all-start.11 = ((f32[16,1,2]{2,1,0:T(1,128)}), f32[16,1,2]{2,1,0:T(1,128)S(1)}, u32[]{:S(2)}, u32[]{:S(2)}) async-start(f32[16,1,2]{2,1,0:T(1,128)} %broadcast_in_dim.53), calls=%async_computation.11 | async-start | bytes 16384 | tf_op jit(solution)/shard_map/all_to_all | solution.py:50
  485.9 10.9 %all-to-all-start.10 = ((f32[16,1,2]{2,1,0:T(1,128)}), f32[16,1,2]{2,1,0:T(1,128)S(1)}, u32[]{:S(2)}, u32[]{:S(2)}) async-start(f32[16,1,2]{2,1,0:T(1,128)} %broadcast_in_dim.52), calls=%async_computation.10 | async-start | bytes 16384 | tf_op jit(solution)/shard_map/all_to_all | solution.py:50
  499.5 10.1 %collective-permute-start.45 = (f32[1,512]{1,0:T(1,128)S(1)}, f32[1,512]{1,0:T(1,128)S(1)}, u32[]{:S(2)}, u32[]{:S(2)}) collective-permute-start(f32[1,512]{1,0:T(1,128)S(1)} %get-tuple-element.263), channel_id=1, source_target_pairs={{0,4},{4,8},{8,12},{12,0},{1,5},{5,9},{9,13},{13,1},{2,6},{6,10},{... | collective-permute-start | bytes 6152 | tf_op jit(solution)/shard_map/ppermute | solution.py:36
  500.1 9.4 %collective-permute-start.46 = (f32[1,512]{1,0:T(1,128)S(1)}, f32[1,512]{1,0:T(1,128)S(1)}, u32[]{:S(2)}, u32[]{:S(2)}) collective-permute-start(f32[1,512]{1,0:T(1,128)S(1)} %get-tuple-element.262), channel_id=1, source_target_pairs={{4,0},{8,4},{12,8},{0,12},{5,1},{9,5},{13,9},{1,13},{6,2},{10,6},{... | collective-permute-start | bytes 6152 | tf_op jit(solution)/shard_map/ppermute | solution.py:37
  512.4 10.9 %all-to-all-start.12 = ((f32[16,1,2]{2,1,0:T(1,128)}), f32[16,1,2]{2,1,0:T(1,128)S(1)}, u32[]{:S(2)}, u32[]{:S(2)}) async-start(f32[16,1,2]{2,1,0:T(1,128)} %broadcast_in_dim.54), calls=%async_computation.12 | async-start | bytes 16384 | tf_op jit(solution)/shard_map/all_to_all | solution.py:50
  527.3 10.1 %collective-permute-start.49 = (f32[1,512]{1,0:T(1,128)S(1)}, f32[1,512]{1,0:T(1,128)S(1)}, u32[]{:S(2)}, u32[]{:S(2)}) collective-permute-start(f32[1,512]{1,0:T(1,128)S(1)} %get-tuple-element.259), channel_id=1, source_target_pairs={{0,4},{4,8},{8,12},{12,0},{1,5},{5,9},{9,13},{13,1},{2,6},{6,10},{... | collective-permute-start | bytes 6152 | tf_op jit(solution)/shard_map/ppermute | solution.py:36
  551.8 10.1 %collective-permute-start.53 = (f32[1,512]{1,0:T(1,128)S(1)}, f32[1,512]{1,0:T(1,128)S(1)}, u32[]{:S(2)}, u32[]{:S(2)}) collective-permute-start(f32[1,512]{1,0:T(1,128)S(1)} %get-tuple-element.255), channel_id=1, source_target_pairs={{0,4},{4,8},{8,12},{12,0},{1,5},{5,9},{9,13},{13,1},{2,6},{6,10},{... | collective-permute-start | bytes 6152 | tf_op jit(solution)/shard_map/ppermute | solution.py:36
  552.5 9.4 %collective-permute-start.54 = (f32[1,512]{1,0:T(1,128)S(1)}, f32[1,512]{1,0:T(1,128)S(1)}, u32[]{:S(2)}, u32[]{:S(2)}) collective-permute-start(f32[1,512]{1,0:T(1,128)S(1)} %get-tuple-element.254), channel_id=1, source_target_pairs={{4,0},{8,4},{12,8},{0,12},{5,1},{9,5},{13,9},{1,13},{6,2},{10,6},{... | collective-permute-start | bytes 6152 | tf_op jit(solution)/shard_map/ppermute | solution.py:37
  564.8 10.9 %all-to-all-start.14 = ((f32[16,1,2]{2,1,0:T(1,128)}), f32[16,1,2]{2,1,0:T(1,128)S(1)}, u32[]{:S(2)}, u32[]{:S(2)}) async-start(f32[16,1,2]{2,1,0:T(1,128)} %broadcast_in_dim.56), calls=%async_computation.14 | async-start | bytes 16384 | tf_op jit(solution)/shard_map/all_to_all | solution.py:50
  579.7 10.1 %collective-permute-start.57 = (f32[1,512]{1,0:T(1,128)S(1)}, f32[1,512]{1,0:T(1,128)S(1)}, u32[]{:S(2)}, u32[]{:S(2)}) collective-permute-start(f32[1,512]{1,0:T(1,128)S(1)} %get-tuple-element.251), channel_id=1, source_target_pairs={{0,4},{4,8},{8,12},{12,0},{1,5},{5,9},{9,13},{13,1},{2,6},{6,10},{... | collective-permute-start | bytes 6152 | tf_op jit(solution)/shard_map/ppermute | solution.py:36
  604.2 10.1 %collective-permute-start.61 = (f32[1,512]{1,0:T(1,128)S(1)}, f32[1,512]{1,0:T(1,128)S(1)}, u32[]{:S(2)}, u32[]{:S(2)}) collective-permute-start(f32[1,512]{1,0:T(1,128)S(1)} %get-tuple-element.247), channel_id=1, source_target_pairs={{0,4},{4,8},{8,12},{12,0},{1,5},{5,9},{9,13},{13,1},{2,6},{6,10},{... | collective-permute-start | bytes 6152 | tf_op jit(solution)/shard_map/ppermute | solution.py:36
  617.1 10.9 %all-to-all-start.16 = ((f32[16,1,2]{2,1,0:T(1,128)}), f32[16,1,2]{2,1,0:T(1,128)S(1)}, u32[]{:S(2)}, u32[]{:S(2)}) async-start(f32[16,1,2]{2,1,0:T(1,128)} %broadcast_in_dim.58), calls=%async_computation.16 | async-start | bytes 16384 | tf_op jit(solution)/shard_map/all_to_all | solution.py:50
  (78 other events, 517.1 us)
where the time goes:
time: 639 us; the launch traced here: 633 us
  starting transfers between devices  195 us (31%)
  waiting for transfers between devices  175 us (27%)
  blocking collectives  133 us (21%)
  other arithmetic  59.7 us (9%)
  between operations  38.7 us (6%)
  local copies, waits for them, and re-layouts  22.3 us (3%)
  loops' own time  8.74 us (1%)
    all_to_all x12, blocking collectives, copy_for_each(): lax.all_to_all(jnp.broadcast_to(array[None], (size, *array.shape)), axis,...  133 us
    ppermute x42, starting transfers between devices, extended(): lax.ppermute(initial, axis, [(b, a) for a, b in up])  93.6 us
    all_to_all x11, waiting for transfers between devices, copy_for_each(): lax.all_to_all(jnp.broadcast_to(array[None], (size, *array.shape)), axis,...  73.1 us
    ppermute x42, waiting for transfers between devices, extended(): lax.ppermute(last, axis, up)  48 us
    all_to_all x11, starting transfers between devices, copy_for_each(): lax.all_to_all(jnp.broadcast_to(array[None], (size, *array.shape)), axis,...  44.1 us
    ppermute x42, starting transfers between devices, extended(): lax.ppermute(last, axis, up)  37.6 us
    concatenate x23, other arithmetic, together(): so_far = over_copies(jnp.concatenate([a.ravel() for a in arrays]), axis)  29.9 us
    ppermute x7, waiting for transfers between devices, shifted(): return lax.ppermute(array, axis, pairs)  27.1 us
  transfers between devices with their start and end apart: 106, of which 53 were waited for; matrix products, arithmetic and copies ran while one was open for 1% of the time, Pallas kernels for 0%

commit v1 on v0

v1 whole, which is shorter than its diff:
```python
import functools

import jax
import jax.numpy as jnp
from jax import lax
from jax.experimental import pallas as pl
from jax.experimental.pallas import tpu as pltpu
from jax.sharding import PartitionSpec as P

FS = 4
EPS = 1e-6
MESH = pl.DeviceIdType.MESH

TILES, ROWS, LANES = 5, 160, 128
TOP, LOW, END = 8, 16, 144
FULL = ((8, 48), (56, 48), (104, 48))
OWN = ((16, 64), (80, 64))
DM, CG, G3, G2, G1, G0 = range(6)


def lane_iota(shape):
    return lax.broadcasted_iota(jnp.int32, shape, len(shape) - 1)


def sides(ref, row, count):
    v = ref[:, row : row + count, :]
    down = ref[:, row + 1 : row + 1 + count, :]
    up = ref[:, row - 1 : row - 1 + count, :]
    lane = lane_iota(v.shape)
    ahead = pltpu.roll(v, LANES - 1, 2)
    right = jnp.where(lane == LANES - 1, jnp.concatenate([ahead[1:], ahead[:1]], 0), ahead)
    behind = pltpu.roll(v, 1, 2)
    left = jnp.where(lane == 0, jnp.concatenate([behind[-1:], behind[:-1]], 0), behind)
    return v, right, left, down, up


def spread(ref, coef, row, count):
    v, right, left, down, up = sides(ref, row, count)
    part = slice(row, row + count)
    out = coef[0, :, part, :] * (v - right) + coef[1, :, part, :] * (v - left)
    out = out + coef[2, :, part, :] * (v - down) + coef[3, :, part, :] * (v - up)
    return v, out


def own_part(x, row, count):
    first, last = max(row, LOW) - row, min(row + count, END) - row
    return x[:4, first:last, :]


def fold(x):
    return jnp.sum(x.reshape(-1, 8, LANES), axis=0)


class Sums:
    def __init__(self):
        self.terms = {}

    def add(self, key, a, b):
        value = fold(a * b)
        self.terms[key] = value if key not in self.terms else self.terms[key] + value


def fine_coefs(m):
    den = m[0] + m[1] + EPS
    alpha = m[0] / den
    gamma = (m[1] + EPS) / den
    s1 = jnp.maximum(
        gamma * gamma * m[0] - 2.0 * gamma * alpha * m[1] + alpha * alpha * m[2], 0.0
    )
    beta = s1 / (m[0] + EPS)
    f = gamma + beta
    pp = s1 + beta * (2.0 * EPS * alpha + beta * m[0])
    plp = jnp.maximum(f * f * m[1] - 2.0 * f * alpha * m[2] + alpha * alpha * m[3], 0.0)
    later = jnp.minimum(s1 / (pp + plp + EPS), 1.0)
    return alpha + later * f, -alpha * later


def kernel(
    forcing, depth, mask, guess, out,
    F, K, V, X, U, W, LG, TG, UG, WG, DEP, MSK, OUT, KAP, ROW,
    PKS, PKR, CKS, CKR, PT, MSG, AR,
    in_sem, hs, hr, ar_s, ar_r, ts, tr, tps, tpr, fs, fps, out_sem,
):
    tm = lax.axis_index("tm")
    lat = lax.axis_index("lat")
    lon = lax.axis_index("lon")
    me = lat * 4 + lon
    chip, core = tm // 2, tm % 2
    sib = 2 * chip + 1 - core

    def cols(c):
        return pl.ds(LANES * c, LANES)

    loads = []
    own_rows = pl.ds(LOW, END - LOW)

    def load(src, dst, field, c):
        copy = pltpu.make_async_copy(src, dst, in_sem.at[field, c])
        copy.start()
        loads.append(copy)

    for c in range(4):
        load(depth.at[:, cols(c)], DEP.at[c], 0, c)
        load(mask.at[:, cols(c)], MSK.at[c], 1, c)
    for c in range(4):
        load(guess.at[0, :, cols(c)], F.at[CG, c, own_rows, :], 2, c)
    for field, level in ((G3, 3), (G2, 2), (G1, 1), (G0, 0)):
        for c in range(4):
            load(forcing.at[level, :, cols(c)], F.at[field, c, own_rows, :], 3 + level, c)

    barrier = pltpu.get_barrier_semaphore()

    def greet(step, _):
        there = lax.rem(me + step, 16)
        pl.semaphore_signal(
            barrier, inc=1, device_id={"lat": there // 4, "lon": there % 4}, device_id_type=MESH
        )
        return 0

    lax.fori_loop(1, 16, greet, 0)
    for step in (2, 4, 6):
        pl.semaphore_signal(
            barrier, inc=1, device_id={"tm": lax.rem(tm + step, 8)}, device_id_type=MESH
        )
    pl.semaphore_signal(barrier, inc=1, device_id={"tm": sib}, device_id_type=MESH)

    def clear(ref):
        zero = jnp.zeros((TILES, 8, LANES), jnp.float32)
        ref[:, 0:8, :] = zero
        ref[:, 152:160, :] = zero

    def clear_fields(i, _):
        clear(F.at[i])
        return 0

    lax.fori_loop(0, 6, clear_fields, 0)
    for ref in (V, X, U):
        clear(ref)

    def clear_slab(i, _):
        clear(TG.at[i])

        @pl.when(i <= tm)
        def _():
            TG[i, :, TOP:152, :] = jnp.zeros((TILES, 144, LANES), jnp.float32)

        ROW[:, i] = jnp.zeros((4, 8, LANES), jnp.float32)
        return 0

    lax.fori_loop(0, 8, clear_slab, 0)

    for copy in loads:
        copy.wait()
    for c in range(4):
        F[DM, c, LOW:END, :] = jnp.where(MSK[c] > 0, DEP[c], 0.0)

    lane6 = lane_iota((6, 8, LANES))
    right_edge = jnp.zeros((6, 8, LANES), jnp.float32)
    left_edge = jnp.zeros((6, 8, LANES), jnp.float32)
    for t in range(16):
        here = (lane6 >= 8 * t) & (lane6 < 8 * t + 8)
        rows = slice(LOW + 8 * t, LOW + 8 * t + 8)
        right_edge = jnp.where(here, pltpu.roll(F[:, 3, rows, :], (8 * t + 8) % LANES, 2), right_edge)
        left_edge = jnp.where(here, pltpu.roll(F[:, 0, rows, :], 8 * t, 2), left_edge)
    PKS[0] = right_edge
    PKS[1] = left_edge
    lane1 = lane_iota((8, LANES))
    corners = ((136, 3, 8), (136, 0, 0), (16, 3, 8), (16, 0, 0))
    for i, (row, tile, shift) in enumerate(corners):
        packed = jnp.zeros((8, LANES), jnp.float32)
        for f in range(6):
            here = (lane1 >= 8 * f) & (lane1 < 8 * f + 8)
            edge = pltpu.roll(F[f, tile, row : row + 8, :], (8 * f + shift) % LANES, 1)
            packed = jnp.where(here, edge, packed)
        CKS[i] = packed

    pl.semaphore_wait(barrier, 19)

    north, south = lax.rem(lat + 3, 4), lax.rem(lat + 1, 4)
    west, east = lax.rem(lon + 3, 4), lax.rem(lon + 1, 4)
    halos = []

    def push(src, dst, i, target):
        copy = pltpu.make_async_remote_copy(
            src, dst, hs.at[i], hr.at[i], device_id=target, device_id_type=MESH
        )
        copy.start()
        halos.append(copy)

    targets = ((south, east), (south, west), (north, east), (north, west))
    for i, (a, b) in enumerate(targets):
        push(CKS.at[i], CKR.at[i], i, {"lat": a, "lon": b})
    push(PKS.at[0], PKR.at[0], 4, {"lon": east})
    push(PKS.at[1], PKR.at[1], 5, {"lon": west})
    for i, first in ((6, 0), (8, 3)):
        group = pl.ds(first, 3)
        push(
            F.at[group, pl.ds(0, 4), pl.ds(136, 8), :],
            F.at[group, pl.ds(0, 4), pl.ds(8, 8), :],
            i, {"lat": south},
        )
        push(
            F.at[group, pl.ds(0, 4), pl.ds(16, 8), :],
            F.at[group, pl.ds(0, 4), pl.ds(144, 8), :],
            i + 1, {"lat": north},
        )
    for copy in halos:
        copy.wait_recv()

    from_left, from_right = PKR[0], PKR[1]
    for t in range(16):
        rows = slice(LOW + 8 * t, LOW + 8 * t + 8)
        a = pltpu.roll(from_left, (120 - 8 * t) % LANES, 2)
        b = pltpu.roll(from_right, (LANES - 8 * t) % LANES, 2)
        F[:, 4, rows, :] = jnp.where(lane6 >= 120, a, jnp.where(lane6 < 8, b, 0.0))
    for row, left, right in ((8, 0, 1), (144, 2, 3)):
        a0, b0 = CKR[left], CKR[right]
        for f in range(6):
            a = pltpu.roll(a0, (120 - 8 * f) % LANES, 1)
            b = pltpu.roll(b0, (LANES - 8 * f) % LANES, 1)
            F[f, 4, row : row + 8, :] = jnp.where(lane1 >= 120, a, jnp.where(lane1 < 8, b, 0.0))

    inside_top = jnp.where(lat > 0, 1.0, 0.0).astype(jnp.float32)
    inside_end = jnp.where(lat < 3, 1.0, 0.0).astype(jnp.float32)
    F[DM, :, 8:16, :] = F[DM, :, 8:16, :] * inside_top
    F[DM, :, 144:152, :] = F[DM, :, 144:152, :] * inside_end

    for row, count in FULL:
        d, *around = sides(F.at[DM], row, count)
        for i, other in enumerate(around):
            K[i, :, row : row + count, :] = jnp.where(
                (d > 0.0) & (other > 0.0), 1.5 * (d + other), 0.0
            )

    def send_sums(r, message):
        MSG[r] = message
        AR[r, me] = message

        def one(step, _):
            there = lax.rem(me + step, 16)
            pltpu.make_async_remote_copy(
                MSG.at[r], AR.at[r, me], ar_s.at[r], ar_r.at[r],
                device_id={"lat": there // 4, "lon": there % 4}, device_id_type=MESH,
            ).start()
            return 0

        lax.fori_loop(1, 16, one, 0)

    def recv_sums(r):
        box = AR.at[r, pl.ds(0, 15)]
        pltpu.make_async_copy(box, box, ar_r.at[r]).wait()
        return jnp.sum(AR[r], axis=0)

    def rows_of(accs):
        row = lax.broadcasted_iota(jnp.int32, (16, LANES), 0)
        stacked = jnp.zeros((16, LANES), jnp.float32)
        for i, acc in enumerate(accs):
            stacked = jnp.where(row == i, jnp.sum(acc, axis=0, keepdims=True), stacked)
        return jnp.broadcast_to(jnp.sum(stacked, axis=1, keepdims=True), (16, LANES))

    def prepare(field, slot):
        sums = Sums()
        for row, count in FULL:
            g, lg = spread(F.at[field], K, row, count)
            LG[slot, :, row : row + count, :] = lg
            g, lg = own_part(g, row, count), own_part(lg, row, count)
            sums.add(0, g, g)
            sums.add(1, g, lg)
            sums.add(2, lg, lg)
        for row, count in OWN:
            lg, llg = spread(LG.at[slot], K, row, count)
            sums.add(3, lg[:4], llg[:4])
        for i in range(4):
            KAP[slot, i] = sums.terms[i]

    def two_steps(r, v_ref, field, slot, between):
        sums = Sums()
        for row, count in FULL:
            v, u = spread(v_ref, K, row, count)
            U[:, row : row + count, :] = u
            g = own_part(F[field, :, row : row + count, :], row, count)
            v, u = own_part(v, row, count), own_part(u, row, count)
            sums.add("m0", v, v)
            sums.add("m1", v, u)
            sums.add("m2", u, u)
            sums.add("n0", v, g)
            sums.add("n1", u, g)
        for row, count in FULL:
            u, w = spread(U, K, row, count)
            W[:, row : row + count, :] = w
            lg = own_part(LG[slot, :, row : row + count, :], row, count)
            u, w = own_part(u, row, count), own_part(w, row, count)
            sums.add("m3", u, w)
            sums.add("m4", w, w)
            sums.add("n2", u, lg)
            sums.add("n3", w, lg)
        for row, count in OWN:
            w, lw = spread(W, K, row, count)
            lg = LG[slot, :4, row : row + count, :]
            sums.add("m5", w[:4], lw[:4])
            sums.add("n4", lw[:4], lg)
        names = ["m0", "m1", "m2", "m3", "m4", "m5", "n0", "n1", "n2", "n3", "n4"]
        accs = [sums.terms[n] for n in names] + [KAP[slot, i] for i in range(4)]
        send_sums(r, rows_of(accs))
        between()
        total = recv_sums(r)
        at = [total[i : i + 1, :] for i in range(15)]
        m, n, k = at[:6], at[6:11], at[11:]
        a, b = fine_coefs(m)
        later = [
            jnp.maximum(
                a * a * m[i] + 2.0 * a * b * m[i + 1] + b * b * m[i + 2]
                + 2.0 * (a * n[i] + b * n[i + 1]) + k[i],
                0.0,
            )
            for i in range(4)
        ]
        a2, b2 = fine_coefs(later)
        return m, (a, b), (a2 * a, a2 * b + b2 * a, b2 * b, a2, b2)

    def scaled(s, x):
        return jnp.broadcast_to(s.reshape(1, 1, LANES), x.shape) * x

    prepare(G3, 0)
    m_start, _, c = two_steps(0, F.at[CG], G3, 0, lambda: prepare(G1, 1))
    for row, count in FULL:
        part = slice(row, row + count)
        X[:, part, :] = (
            scaled(c[0], F[CG, :, part, :]) + scaled(c[1], U[:, part, :]) + scaled(c[2], W[:, part, :])
            + scaled(c[3], F[G3, :, part, :]) + scaled(c[4], LG[0, :, part, :]) + F[G2, :, part, :]
        )
    last = jnp.where(tm == 7, 1.0, 0.0).astype(jnp.float32)
    psi = m_start[0] / (m_start[0] + 4.0 * m_start[1] + EPS)
    drop = psi * (last - 1.0)

    _, _, c = two_steps(1, X, G1, 1, lambda: prepare(G2, 2))
    for row, count in FULL:
        part = slice(row, row + count)
        TG[tm, :, part, :] = (
            scaled(c[0], X[:, part, :]) + scaled(c[1], U[:, part, :]) + scaled(c[2], W[:, part, :])
            + scaled(c[3], F[G1, :, part, :]) + scaled(c[4], LG[1, :, part, :]) + F[G0, :, part, :]
            + scaled(drop, F[CG, :, part, :])
        )

    lane2 = lane_iota((8, LANES))
    for half in range(2):
        packed = jnp.zeros((8, LANES), jnp.float32)
        for t in range(9):
            row = TOP + 8 * (9 * half + t)
            here = (lane2 >= 8 * t) & (lane2 < 8 * t + 8)
            packed = jnp.where(here, pltpu.roll(TG[tm, 4, row : row + 8, :], 8 * t + 4, 1), packed)
        PT[tm, 8 * half : 8 * half + 8, :] = packed

    def slab_copies(k, s_main, s_pack, target):
        main = TG.at[k, pl.ds(0, 4), pl.ds(TOP, 144), :]
        return (
            pltpu.make_async_remote_copy(
                main, main, s_main, tr.at[k], device_id={"tm": target}, device_id_type=MESH
            ),
            pltpu.make_async_remote_copy(
                PT.at[k], PT.at[k], s_pack, tpr.at[k], device_id={"tm": target}, device_id_type=MESH
            ),
        )

    def each_send(act):
        @pl.when(core == 1)
        def _():
            for copy in slab_copies(tm, ts.at[0], tps.at[0], sib):
                act(copy)

        for dx in (1, 3, 2):
            @pl.when(chip >= dx)
            def _():
                for copy in slab_copies(tm, ts.at[dx], tps.at[dx], jnp.maximum(tm - 2 * dx, 0)):
                    act(copy)

    each_send(lambda copy: copy.start())

    def slab_at(e):
        h = (e + 1) // 2
        dx = jnp.where(h == 1, 1, jnp.where(h == 2, 3, 2))
        same = e % 2
        k = jnp.where(e == 0, tm + 1, jnp.where(same == 1, tm, sib) + 2 * dx)
        valid = jnp.where(e == 0, core == 0, chip + dx <= 3)
        return jnp.minimum(k, 7), dx, valid

    def arrive(e, _):
        k, dx, valid = slab_at(e)

        @pl.when(valid)
        def _():
            for copy in slab_copies(k, ts.at[0], tps.at[0], sib):
                copy.wait_recv()

            @pl.when(e % 2 == 1)
            def _():
                for copy in slab_copies(k, fs.at[dx], fps.at[dx], sib):
                    copy.start()

            for half in range(2):
                packed = PT[k, 8 * half : 8 * half + 8, :]
                for t in range(9):
                    row = TOP + 8 * (9 * half + t)
                    back = pltpu.roll(packed, (LANES - 8 * t - 4) % LANES, 1)
                    TG[k, 4, row : row + 8, :] = jnp.where((lane2 < 4) | (lane2 >= 124), back, 0.0)
            for row, count in FULL:
                _, u = spread(TG.at[k], K, row, count)
                UG[k, :, row : row + count, :] = u
            for row, count in OWN:
                _, w = spread(UG.at[k], K, row, count)
                WG[:, row - LOW : row - LOW + count, :] = w[:4]

            def pair(q, _):
                j, _, held = slab_at(q)

                @pl.when(held)
                def _():
                    sums = Sums()
                    for t in range(4):
                        tk, uk, wk = TG[k, t, LOW:END, :], UG[k, t, LOW:END, :], WG[t]
                        tj, uj = TG[j, t, LOW:END, :], UG[j, t, LOW:END, :]
                        sums.add(0, tj, tk)
                        sums.add(1, tj, uk)
                        sums.add(2, uj, uk)
                        sums.add(3, uj, wk)
                    for i in range(4):
                        value = jnp.sum(sums.terms[i], axis=0, keepdims=True)
                        ROW[i, k, pl.ds(j, 1), :] = value
                        ROW[i, j, pl.ds(k, 1), :] = value

                return 0

            lax.fori_loop(0, e + 1, pair, 0)

        return 0

    lax.fori_loop(0, 7, arrive, 0)

    lane3 = lane_iota((8, 8, LANES))
    sub3 = lax.broadcasted_iota(jnp.int32, (8, 8, LANES), 1)
    gram = jnp.zeros((8, 8, LANES), jnp.float32)
    for i in range(4):
        gram = jnp.where(lane3 == 8 * i + sub3, jnp.sum(ROW[i], axis=2, keepdims=True), gram)
    gram = jnp.sum(gram, axis=1)
    send_sums(2, jnp.concatenate([gram, jnp.zeros((8, LANES), jnp.float32)], 0))
    total = recv_sums(2)[:8]

    lane = lane_iota((8, LANES))
    table = [
        [
            None if j == 0 else jnp.broadcast_to(
                jnp.sum(jnp.where(lane == 8 * i + j, total, 0.0), axis=1, keepdims=True), (8, LANES)
            )
            for j in range(8)
        ]
        for i in range(4)
    ]

    def entry(i, k, j):
        return table[i][j][k : k + 1, :]

    one = jnp.ones((1, LANES), jnp.float32)
    zero = jnp.zeros((1, LANES), jnp.float32)
    coefs = {7: one}
    quad = [entry(i, 7, 7) for i in range(4)]
    cross = [{j: entry(i, 7, j) for j in range(1, 7)} for i in range(4)]
    is_last = jnp.full((1, LANES), tm == 7)
    held_c = {k: zero for k in range(1, 8)}
    held_q = [m_start[i] for i in range(4)]
    for t in range(7, 0, -1):
        if t < 7:
            psi_t = quad[0] / (quad[0] + 4.0 * quad[1] + EPS)
            quad = [
                psi_t * psi_t * quad[i] + 2.0 * psi_t * cross[i][t] + entry(i, t, t)
                for i in range(4)
            ]
            cross = [{j: psi_t * cross[i][j] + entry(i, t, j) for j in range(1, t)} for i in range(4)]
            coefs = {k: psi_t * x for k, x in coefs.items()}
            coefs[t] = one
        now = jnp.full((1, LANES), tm + 1 == t)
        for k in coefs:
            held_c[k] = jnp.where(now, coefs[k], held_c[k])
        held_q = [jnp.where(now, quad[i], held_q[i]) for i in range(4)]
    psi = held_q[0] / (held_q[0] + 4.0 * held_q[1] + EPS)
    psi = jnp.where(is_last, 0.0, psi)
    for row, count in FULL:
        part = slice(row, row + count)
        value = F[CG, :, part, :] * last
        for k in range(1, 8):
            value = value + scaled(held_c[k], TG[k, :, part, :])
        V[:, part, :] = value

    outs = []

    def put(level):
        for c in range(4):
            copy = pltpu.make_async_copy(
                OUT.at[level, c], out.at[level, :, cols(c)], out_sem.at[level, c]
            )
            copy.start()
            outs.append(copy)

    a, b = fine_coefs(held_q)
    for row, count in FULL:
        part = slice(row, row + count)
        v, u = spread(V, K, row, count)
        value = scaled(a, v) + scaled(b, u) + F[G3, :, part, :]
        X[:, part, :] = value
        first, end = max(row, LOW) - LOW, min(row + count, END) - LOW
        OUT[3, :, first:end, :] = own_part(value, row, count)
    put(3)

    def write_first():
        for row, count in OWN:
            part = slice(row, row + count)
            value = scaled(psi, V[:4, part, :]) + TG[tm, :4, part, :]
            OUT[0, :, row - LOW : row - LOW + count, :] = value
        put(0)

    _, (a, b), c = two_steps(3, X, G2, 2, write_first)
    for row, count in OWN:
        part = slice(row, row + count)
        inner = slice(row - LOW, row - LOW + count)
        v, u, w = X[:4, part, :], U[:4, part, :], W[:4, part, :]
        g = F[G2, :4, part, :]
        OUT[2, :, inner, :] = scaled(a, v) + scaled(b, u) + g
        OUT[1, :, inner, :] = (
            scaled(c[0], v) + scaled(c[1], u) + scaled(c[2], w) + scaled(c[3], g)
            + scaled(c[4], LG[2, :4, part, :]) + F[G1, :4, part, :]
        )
    put(2)
    put(1)

    for copy in halos:
        copy.wait_send()
    for r in range(4):
        box = AR.at[r, pl.ds(0, 15)]
        pltpu.make_async_copy(box, box, ar_s.at[r]).wait()
    each_send(lambda copy: copy.wait_send())
    for dx in (1, 3, 2):
        @pl.when(chip + dx <= 3)
        def _():
            for copy in slab_copies(jnp.minimum(tm + 2 * dx, 7), fs.at[dx], fps.at[dx], sib):
                copy.wait_send()
    for copy in outs:
        copy.wait()


def local(forcing, depth, mask, guess):
    f32 = jnp.float32
    field = (TILES, ROWS, LANES)
    dma = pltpu.SemaphoreType.DMA
    return pl.pallas_call(
        kernel,
        out_shape=jax.ShapeDtypeStruct(forcing.shape, f32),
        in_specs=[pl.BlockSpec(memory_space=pl.ANY)] * 4,
        out_specs=pl.BlockSpec(memory_space=pl.ANY),
        scratch_shapes=[
            pltpu.VMEM((6, *field), f32),
            pltpu.VMEM((4, *field), f32),
            pltpu.VMEM(field, f32),
            pltpu.VMEM(field, f32),
            pltpu.VMEM(field, f32),
            pltpu.VMEM(field, f32),
            pltpu.VMEM((3, *field), f32),
            pltpu.VMEM((8, *field), f32),
            pltpu.VMEM((8, *field), f32),
            pltpu.VMEM((4, 128, LANES), f32),
            pltpu.VMEM((4, 128, LANES), f32),
            pltpu.VMEM((4, 128, LANES), jnp.int32),
            pltpu.VMEM((4, 4, 128, LANES), f32),
            pltpu.VMEM((3, 4, 8, LANES), f32),
            pltpu.VMEM((4, 8, 8, LANES), f32),
            pltpu.VMEM((2, 6, 8, LANES), f32),
            pltpu.VMEM((2, 6, 8, LANES), f32),
            pltpu.VMEM((4, 8, LANES), f32),
            pltpu.VMEM((4, 8, LANES), f32),
            pltpu.VMEM((8, 16, LANES), f32),
            pltpu.VMEM((4, 16, LANES), f32),
            pltpu.VMEM((4, 16, 16, LANES), f32),
            dma((7, 4)),
            dma((10,)),
            dma((10,)),
            dma((4,)),
            dma((4,)),
            dma((4,)),
            dma((8,)),
            dma((4,)),
            dma((8,)),
            dma((4,)),
            dma((4,)),
            dma((4, 4)),
        ],
        compiler_params=pltpu.CompilerParams(
            collective_id=0, has_side_effects=True, vmem_limit_bytes=48 * 1024 * 1024
        ),
        name="cycle",
    )(forcing, depth, mask, guess)


def solution(mesh):
    return jax.shard_map(
        local,
        mesh=mesh,
        in_specs=(P("tm", "lat", "lon"), P("lat", "lon"), P("lat", "lon"), P("tm", "lat", "lon")),
        out_specs=P("tm", "lat", "lon"),
        check_vma=False,
    )
```

time: 639 us -> 62.3 us (0.10)
  the two profiles are of different devices: /device:TPU:2 before, /device:TPU:1 now
where the time goes in v1:
time: 62.3 us; the launch traced here: 61.2 us
  Pallas kernels  56.1 us (90%)
  local copies, waits for them, and re-layouts  5.05 us (8%)
    pallas_call x1, Pallas kernels, local(): pl.pallas_call(kernel, out_shape=jax.ShapeDtypeStruct(forcing.shape, f32)...  56.1 us
    unnamed x9, local copies, waits for them, and re-layouts  5.05 us

profile of v1, /device:TPU:1, one launch (start us, length us, event | category | flops | bytes accessed | tf_op | source)
XLA Modules:
  0.0 61.2 jit_solution(12872539738555640989)
XLA Ops:
  0.0 0.0 copy-start
  0.0 1.2 %copy-done = f32[4,128,512]{2,1,0:T(8,128)S(1)} copy-done((f32[4,128,512]{2,1,0:T(8,128)S(1)}, f32[4,128,512]{2,1,0:T(8,128)}, u32[]{:S(2)}) %copy-start) | copy-done | bytes 1048600
  1.2 0.0 copy-start.1
  1.2 0.9 %copy-done.1 = f32[128,512]{1,0:T(8,128)S(1)} copy-done((f32[128,512]{1,0:T(8,128)S(1)}, f32[128,512]{1,0:T(8,128)}, u32[]{:S(2)}) %copy-start.1) | copy-done | bytes 262168
  2.2 0.0 copy-start.2
  2.2 0.9 %copy-done.2 = s32[128,512]{1,0:T(8,128)S(1)} copy-done((s32[128,512]{1,0:T(8,128)S(1)}, s32[128,512]{1,0:T(8,128)}, u32[]{:S(2)}) %copy-start.2) | copy-done | bytes 262168
  3.1 0.0 copy-start.3
  3.1 0.9 %copy-done.3 = f32[1,128,512]{2,1,0:T(8,128)S(1)} copy-done((f32[1,128,512]{2,1,0:T(8,128)S(1)}, f32[1,128,512]{2,1,0:T(8,128)}, u32[]{:S(2)}) %copy-start.3) | copy-done | bytes 262168
  4.1 56.1 %cycle.1 = f32[4,128,512]{2,1,0:T(8,128)S(1)} custom-call(f32[4,128,512]{2,1,0:T(8,128)S(1)} %copy-done, f32[128,512]{1,0:T(8,128)S(1)} %copy-done.1, s32[128,512]{1,0:T(8,128)S(1)} %copy-done.2, f32[1,128,512]{2,1,0:T(8,128)S(1)} %copy-done.3), custom_call_target="tpu_custom_call" | custom-call | tf_op jit(solution)/shard_map/cycle/pallas_call | solution.py:553
  60.2 1.0 %copy.6 = f32[4,128,512]{2,1,0:T(8,128)} copy(f32[4,128,512]{2,1,0:T(8,128)S(1)} %cycle.1) | data formatting | bytes 2097152
Async XLA Ops:
  0.0 1.2 %copy-start = (f32[4,128,512]{2,1,0:T(8,128)S(1)}, f32[4,128,512]{2,1,0:T(8,128)}, u32[]{:S(2)}) copy-start(f32[4,128,512]{2,1,0:T(8,128)} %forcing.1) | copy-start | bytes 3145732
  1.2 0.9 %copy-start.1 = (f32[128,512]{1,0:T(8,128)S(1)}, f32[128,512]{1,0:T(8,128)}, u32[]{:S(2)}) copy-start(f32[128,512]{1,0:T(8,128)} %depth.1) | copy-start | bytes 786436
  2.2 0.9 %copy-start.2 = (s32[128,512]{1,0:T(8,128)S(1)}, s32[128,512]{1,0:T(8,128)}, u32[]{:S(2)}) copy-start(s32[128,512]{1,0:T(8,128)} %mask.1) | copy-start | bytes 786436
  3.1 0.9 %copy-start.3 = (f32[1,128,512]{2,1,0:T(8,128)S(1)}, f32[1,128,512]{2,1,0:T(8,128)}, u32[]{:S(2)}) copy-start(f32[1,128,512]{2,1,0:T(8,128)} %guess.1) | copy-start | bytes 786436

commit v2 on v1

--- a/solution.py
+++ b/solution.py
@@ -9,6 +9,7 @@
 
 FS = 4
 EPS = 1e-6
+VMEM_LIMIT = 40 * 1024 * 1024
 MESH = pl.DeviceIdType.MESH
 
 TILES, ROWS, LANES = 5, 160, 128
@@ -49,6 +50,18 @@
 
 def fold(x):
     return jnp.sum(x.reshape(-1, 8, LANES), axis=0)
+
+
+class Phase:
+    def __init__(self):
+        self.open = None
+
+    def __call__(self, name):
+        if self.open is not None:
+            self.open.__exit__(None, None, None)
+        self.open = jax.named_scope(name) if name else None
+        if self.open is not None:
+            self.open.__enter__()
 
 
 class Sums:
@@ -77,10 +90,12 @@
 
 def kernel(
     forcing, depth, mask, guess, out,
-    F, K, V, X, U, W, LG, TG, UG, WG, DEP, MSK, OUT, KAP, ROW,
+    F, K, V, X, U, W, LG, TG, UG, WG, DEP, MSK, KAP, ROW,
     PKS, PKR, CKS, CKR, PT, MSG, AR,
-    in_sem, hs, hr, ar_s, ar_r, ts, tr, tps, tpr, fs, fps, out_sem,
+    in_sem, hs, hr, ar_s, ar_r, ts, tr, tps, tpr, fs, fps,
 ):
+    phase = Phase()
+    phase("a0_load")
     tm = lax.axis_index("tm")
     lat = lax.axis_index("lat")
     lon = lax.axis_index("lon")
@@ -90,6 +105,24 @@
 
     def cols(c):
         return pl.ds(LANES * c, LANES)
+
+    barrier = pltpu.get_barrier_semaphore()
+    north, south = lax.rem(lat + 3, 4), lax.rem(lat + 1, 4)
+    west, east = lax.rem(lon + 3, 4), lax.rem(lon + 1, 4)
+
+    def greet(target):
+        pl.semaphore_signal(barrier, inc=1, device_id=target, device_id_type=MESH)
+
+    for a in (north, south):
+        for b in (west, east):
+            greet({"lat": a, "lon": b})
+    for step in (4, 2, 6):
+        greet({"tm": lax.rem(tm + step, 8)})
+    for a in (north, south):
+        greet({"lat": a})
+    for b in (west, east):
+        greet({"lon": b})
+    greet({"tm": sib})
 
     loads = []
     own_rows = pl.ds(LOW, END - LOW)
@@ -108,22 +141,7 @@
         for c in range(4):
             load(forcing.at[level, :, cols(c)], F.at[field, c, own_rows, :], 3 + level, c)
 
-    barrier = pltpu.get_barrier_semaphore()
-
-    def greet(step, _):
-        there = lax.rem(me + step, 16)
-        pl.semaphore_signal(
-            barrier, inc=1, device_id={"lat": there // 4, "lon": there % 4}, device_id_type=MESH
-        )
-        return 0
-
-    lax.fori_loop(1, 16, greet, 0)
-    for step in (2, 4, 6):
-        pl.semaphore_signal(
-            barrier, inc=1, device_id={"tm": lax.rem(tm + step, 8)}, device_id_type=MESH
-        )
-    pl.semaphore_signal(barrier, inc=1, device_id={"tm": sib}, device_id_type=MESH)
-
+    phase("a1_clear")
     def clear(ref):
         zero = jnp.zeros((TILES, 8, LANES), jnp.float32)
         ref[:, 0:8, :] = zero
@@ -149,11 +167,13 @@
 
     lax.fori_loop(0, 8, clear_slab, 0)
 
+    phase("a2_loadwait")
     for copy in loads:
         copy.wait()
     for c in range(4):
         F[DM, c, LOW:END, :] = jnp.where(MSK[c] > 0, DEP[c], 0.0)
 
+    phase("a3_pack")
     lane6 = lane_iota((6, 8, LANES))
     right_edge = jnp.zeros((6, 8, LANES), jnp.float32)
     left_edge = jnp.zeros((6, 8, LANES), jnp.float32)
@@ -174,10 +194,9 @@
             packed = jnp.where(here, edge, packed)
         CKS[i] = packed
 
-    pl.semaphore_wait(barrier, 19)
-
-    north, south = lax.rem(lat + 3, 4), lax.rem(lat + 1, 4)
-    west, east = lax.rem(lon + 3, 4), lax.rem(lon + 1, 4)
+    phase("a4_barrier")
+    pl.semaphore_wait(barrier, 12)
+
     halos = []
 
     def push(src, dst, i, target):
@@ -204,9 +223,11 @@
             F.at[group, pl.ds(0, 4), pl.ds(144, 8), :],
             i + 1, {"lat": north},
         )
-    for copy in halos:
+    phase("a5_halowait")
+    for copy in halos[:8]:
         copy.wait_recv()
 
+    phase("a6_unpack")
     from_left, from_right = PKR[0], PKR[1]
     for t in range(16):
         rows = slice(LOW + 8 * t, LOW + 8 * t + 8)
@@ -274,6 +295,7 @@
             KAP[slot, i] = sums.terms[i]
 
     def two_steps(r, v_ref, field, slot, between):
+        phase(f"r{r}_moments")
         sums = Sums()
         for row, count in FULL:
             v, u = spread(v_ref, K, row, count)
@@ -302,8 +324,11 @@
         names = ["m0", "m1", "m2", "m3", "m4", "m5", "n0", "n1", "n2", "n3", "n4"]
         accs = [sums.terms[n] for n in names] + [KAP[slot, i] for i in range(4)]
         send_sums(r, rows_of(accs))
+        phase(f"r{r}_between")
         between()
+        phase(f"r{r}_wait")
         total = recv_sums(r)
+        phase(f"r{r}_scalars")
         at = [total[i : i + 1, :] for i in range(15)]
         m, n, k = at[:6], at[6:11], at[11:]
         a, b = fine_coefs(m)
@@ -321,8 +346,15 @@
     def scaled(s, x):
         return jnp.broadcast_to(s.reshape(1, 1, LANES), x.shape) * x
 
+    phase("a7_prepare")
     prepare(G3, 0)
-    m_start, _, c = two_steps(0, F.at[CG], G3, 0, lambda: prepare(G1, 1))
+
+    def rest_of_halo():
+        for copy in halos[8:]:
+            copy.wait_recv()
+        prepare(G1, 1)
+
+    m_start, _, c = two_steps(0, F.at[CG], G3, 0, rest_of_halo)
     for row, count in FULL:
         part = slice(row, row + count)
         X[:, part, :] = (
@@ -342,6 +374,7 @@
             + scaled(drop, F[CG, :, part, :])
         )
 
+    phase("b0_gather")
     lane2 = lane_iota((8, LANES))
     for half in range(2):
         packed = jnp.zeros((8, LANES), jnp.float32)
@@ -389,8 +422,9 @@
 
         @pl.when(valid)
         def _():
-            for copy in slab_copies(k, ts.at[0], tps.at[0], sib):
-                copy.wait_recv()
+            with jax.named_scope("b1_slabwait"):
+                for copy in slab_copies(k, ts.at[0], tps.at[0], sib):
+                    copy.wait_recv()
 
             @pl.when(e % 2 == 1)
             def _():
@@ -434,8 +468,10 @@
 
         return 0
 
+    phase("b1_arrive")
     lax.fori_loop(0, 7, arrive, 0)
 
+    phase("b2_gram")
     lane3 = lane_iota((8, 8, LANES))
     sub3 = lax.broadcasted_iota(jnp.int32, (8, 8, LANES), 1)
     gram = jnp.zeros((8, 8, LANES), jnp.float32)
@@ -443,7 +479,9 @@
         gram = jnp.where(lane3 == 8 * i + sub3, jnp.sum(ROW[i], axis=2, keepdims=True), gram)
     gram = jnp.sum(gram, axis=1)
     send_sums(2, jnp.concatenate([gram, jnp.zeros((8, LANES), jnp.float32)], 0))
+    phase("b3_wait")
     total = recv_sums(2)[:8]
+    phase("b4_chain")
 
     lane = lane_iota((8, LANES))
     table = [
@@ -490,47 +528,37 @@
             value = value + scaled(held_c[k], TG[k, :, part, :])
         V[:, part, :] = value
 
-    outs = []
-
-    def put(level):
-        for c in range(4):
-            copy = pltpu.make_async_copy(
-                OUT.at[level, c], out.at[level, :, cols(c)], out_sem.at[level, c]
-            )
-            copy.start()
-            outs.append(copy)
-
+    def put(level, row, value):
+        for t in range(4):
+            out[level, row - LOW : row - LOW + value.shape[1], cols(t)] = value[t]
+
+    phase("c0_correct")
     a, b = fine_coefs(held_q)
     for row, count in FULL:
         part = slice(row, row + count)
         v, u = spread(V, K, row, count)
         value = scaled(a, v) + scaled(b, u) + F[G3, :, part, :]
         X[:, part, :] = value
-        first, end = max(row, LOW) - LOW, min(row + count, END) - LOW
-        OUT[3, :, first:end, :] = own_part(value, row, count)
-    put(3)
+        put(3, max(row, LOW), own_part(value, row, count))
 
     def write_first():
         for row, count in OWN:
             part = slice(row, row + count)
-            value = scaled(psi, V[:4, part, :]) + TG[tm, :4, part, :]
-            OUT[0, :, row - LOW : row - LOW + count, :] = value
-        put(0)
+            put(0, row, scaled(psi, V[:4, part, :]) + TG[tm, :4, part, :])
 
     _, (a, b), c = two_steps(3, X, G2, 2, write_first)
     for row, count in OWN:
         part = slice(row, row + count)
-        inner = slice(row - LOW, row - LOW + count)
         v, u, w = X[:4, part, :], U[:4, part, :], W[:4, part, :]
         g = F[G2, :4, part, :]
-        OUT[2, :, inner, :] = scaled(a, v) + scaled(b, u) + g
-        OUT[1, :, inner, :] = (
+        put(2, row, scaled(a, v) + scaled(b, u) + g)
+        last_value = (
             scaled(c[0], v) + scaled(c[1], u) + scaled(c[2], w) + scaled(c[3], g)
             + scaled(c[4], LG[2, :4, part, :]) + F[G1, :4, part, :]
         )
-    put(2)
-    put(1)
-
+        put(1, row, last_value)
+
+    phase("c9_end")
     for copy in halos:
         copy.wait_send()
     for r in range(4):
@@ -542,8 +570,7 @@
         def _():
             for copy in slab_copies(jnp.minimum(tm + 2 * dx, 7), fs.at[dx], fps.at[dx], sib):
                 copy.wait_send()
-    for copy in outs:
-        copy.wait()
+    phase(None)
 
 
 def local(forcing, depth, mask, guess):
@@ -553,8 +580,8 @@
     return pl.pallas_call(
         kernel,
         out_shape=jax.ShapeDtypeStruct(forcing.shape, f32),
-        in_specs=[pl.BlockSpec(memory_space=pl.ANY)] * 4,
-        out_specs=pl.BlockSpec(memory_space=pl.ANY),
+        in_specs=[pl.BlockSpec(memory_space=pltpu.HBM)] * 4,
+        out_specs=pl.BlockSpec(memory_space=pltpu.VMEM),
         scratch_shapes=[
             pltpu.VMEM((6, *field), f32),
             pltpu.VMEM((4, *field), f32),
@@ -568,7 +595,6 @@
             pltpu.VMEM((4, 128, LANES), f32),
             pltpu.VMEM((4, 128, LANES), f32),
             pltpu.VMEM((4, 128, LANES), jnp.int32),
-            pltpu.VMEM((4, 4, 128, LANES), f32),
             pltpu.VMEM((3, 4, 8, LANES), f32),
             pltpu.VMEM((4, 8, 8, LANES), f32),
             pltpu.VMEM((2, 6, 8, LANES), f32),
@@ -589,13 +615,12 @@
             dma((8,)),
             dma((4,)),
             dma((4,)),
-            dma((4, 4)),
         ],
         compiler_params=pltpu.CompilerParams(
-            collective_id=0, has_side_effects=True, vmem_limit_bytes=48 * 1024 * 1024
+            collective_id=0, has_side_effects=True, vmem_limit_bytes=VMEM_LIMIT
         ),
         name="cycle",
-    )(forcing, depth, mask, guess)
+    )(*(pltpu.with_memory_space_constraint(x, pltpu.HBM) for x in (forcing, depth, mask, guess)))
 
 
 def solution(mesh):

time: 62.3 us -> 56.7 us (0.910)
  local copies, waits for them, and re-layouts: 5.05 us -> 0.97 us
  Pallas kernels: 56.1 us -> 54.7 us
    unnamed x9 -> x1, local copies, waits for them, and re-layouts: 5.05 us -> 0.97 us
    pallas_call x1, Pallas kernels: 56.1 us -> 54.7 us  [local(): pl.pallas_call(kernel, out_shape=jax.ShapeDtypeStruct(forcing.shape, f32)...]
where the time goes in v2:
time: 56.7 us; the launch traced here: 55.6 us
  Pallas kernels  54.7 us (96%)
  local copies, waits for them, and re-layouts  0.97 us (2%)
    pallas_call x1, Pallas kernels, local(): pl.pallas_call(kernel, out_shape=jax.ShapeDtypeStruct(forcing.shape, f32)...  54.7 us

profile of v2, /device:TPU:1, one launch (start us, length us, event | category | flops | bytes accessed | tf_op | source)
XLA Modules:
  0.0 55.6 jit_solution(18383645514938684676)
XLA Ops:
  0.0 54.7 %cycle.1 = f32[4,128,512]{2,1,0:T(8,128)S(1)} custom-call(f32[4,128,512]{2,1,0:T(8,128)} %forcing.1, f32[128,512]{1,0:T(8,128)} %depth.1, s32[128,512]{1,0:T(8,128)} %mask.1, f32[1,128,512]{2,1,0:T(8,128)} %guess.1), custom_call_target="tpu_custom_call" | custom-call | tf_op jit(solution)/shard_map/cycle/pallas_call | solution.py:580
  54.7 1.0 %copy.6 = f32[4,128,512]{2,1,0:T(8,128)} copy(f32[4,128,512]{2,1,0:T(8,128)S(1)} %cycle.1) | data formatting | bytes 2097152

commit v3 on v2

--- a/solution.py
+++ b/solution.py
@@ -16,6 +16,9 @@
 TOP, LOW, END = 8, 16, 144
 FULL = ((8, 48), (56, 48), (104, 48))
 OWN = ((16, 64), (80, 64))
+HALVES = ((12, 68), (80, 68))
+GRAM_U = (((8, 32), (40, 36)), ((64, 48), (112, 40)))
+GRAM_OWN = (((16, 56),), ((72, 40), (112, 32)))
 DM, CG, G3, G2, G1, G0 = range(6)
 
 
@@ -92,7 +95,7 @@
     forcing, depth, mask, guess, out,
     F, K, V, X, U, W, LG, TG, UG, WG, DEP, MSK, KAP, ROW,
     PKS, PKR, CKS, CKR, PT, MSG, AR,
-    in_sem, hs, hr, ar_s, ar_r, ts, tr, tps, tpr, fs, fps,
+    GM, GR, in_sem, hs, hr, ar_s, ar_r, ts, tr, tpr, fs, rs, gs, gr, plane_sem,
 ):
     phase = Phase()
     phase("a0_load")
@@ -157,11 +160,6 @@
 
     def clear_slab(i, _):
         clear(TG.at[i])
-
-        @pl.when(i <= tm)
-        def _():
-            TG[i, :, TOP:152, :] = jnp.zeros((TILES, 144, LANES), jnp.float32)
-
         ROW[:, i] = jnp.zeros((4, 8, LANES), jnp.float32)
         return 0
 
@@ -227,6 +225,7 @@
     for copy in halos[:8]:
         copy.wait_recv()
 
+    pl.semaphore_signal(plane_sem, inc=1, device_id={"tm": sib}, device_id_type=MESH)
     phase("a6_unpack")
     from_left, from_right = PKR[0], PKR[1]
     for t in range(16):
@@ -384,92 +383,144 @@
             packed = jnp.where(here, pltpu.roll(TG[tm, 4, row : row + 8, :], 8 * t + 4, 1), packed)
         PT[tm, 8 * half : 8 * half + 8, :] = packed
 
-    def slab_copies(k, s_main, s_pack, target):
-        main = TG.at[k, pl.ds(0, 4), pl.ds(TOP, 144), :]
-        return (
+    def half_copies(k, h, sems, target):
+        row, count = HALVES[h]
+        main = TG.at[k, pl.ds(0, 4), pl.ds(row, count), :]
+        pack = PT.at[k, pl.ds(8 * h, 8), :]
+        return [
             pltpu.make_async_remote_copy(
-                main, main, s_main, tr.at[k], device_id={"tm": target}, device_id_type=MESH
-            ),
-            pltpu.make_async_remote_copy(
-                PT.at[k], PT.at[k], s_pack, tpr.at[k], device_id={"tm": target}, device_id_type=MESH
-            ),
-        )
-
-    def each_send(act):
-        @pl.when(core == 1)
-        def _():
-            for copy in slab_copies(tm, ts.at[0], tps.at[0], sib):
-                act(copy)
-
-        for dx in (1, 3, 2):
-            @pl.when(chip >= dx)
+                ref, ref, sems.at[i], recv.at[k, h], device_id={"tm": target}, device_id_type=MESH
+            )
+            for i, (ref, recv) in enumerate(((main, tr), (pack, tpr)))
+        ]
+
+    below, above = jnp.maximum(tm - 2, 0), jnp.minimum(tm + 2, 7)
+    wrapped = lax.rem(tm + 2, 8)
+
+    def own_sends(act):
+        for h in range(2):
+            @pl.when(core == 1)
             def _():
-                for copy in slab_copies(tm, ts.at[dx], tps.at[dx], jnp.maximum(tm - 2 * dx, 0)):
-                    act(copy)
-
-    each_send(lambda copy: copy.start())
+                act(half_copies(tm, h, ts.at[0, h], sib))
+
+            @pl.when(chip == 3)
+            def _():
+                act(half_copies(tm, h, ts.at[1, h], wrapped))
+
+            @pl.when(chip >= 1)
+            def _():
+                act(half_copies(tm, h, ts.at[2, h], below))
+
+            if h == 1:
+                @pl.when(chip == 2)
+                def _():
+                    act(half_copies(tm, h, ts.at[1, h], above))
+
+    def start(copies):
+        for copy in copies:
+            copy.start()
+
+    def sent(copies):
+        for copy in copies:
+            copy.wait_send()
+
+    def landed(copies):
+        for copy in copies:
+            copy.wait_recv()
+
+    own_sends(start)
 
     def slab_at(e):
-        h = (e + 1) // 2
-        dx = jnp.where(h == 1, 1, jnp.where(h == 2, 3, 2))
-        same = e % 2
-        k = jnp.where(e == 0, tm + 1, jnp.where(same == 1, tm, sib) + 2 * dx)
-        valid = jnp.where(e == 0, core == 0, chip + dx <= 3)
-        return jnp.minimum(k, 7), dx, valid
-
-    def arrive(e, _):
-        k, dx, valid = slab_at(e)
-
-        @pl.when(valid)
-        def _():
-            with jax.named_scope("b1_slabwait"):
-                for copy in slab_copies(k, ts.at[0], tps.at[0], sib):
-                    copy.wait_recv()
-
-            @pl.when(e % 2 == 1)
+        dx = jnp.where(e >= 5, 2, jnp.where(e % 2 == 1, 1, 3))
+        same = (e == 1) | (e == 2) | (e == 5)
+        k = jnp.where(e == 0, 2 * chip + 1, jnp.where(same, tm, sib) + 2 * dx)
+        valid = (e == 0) | (chip + dx <= 3)
+        return jnp.minimum(k, 7), dx, same, valid
+
+    def relay_from(e, h):
+        if h == 0:
+            return (e == 1) & ((chip == 1) | (chip == 2)), below
+        return (e == 2) & (chip == 0), above
+
+    def unpack(k, h):
+        packed = PT[k, 8 * h : 8 * h + 8, :]
+        for t in range(9):
+            row = TOP + 8 * (9 * h + t)
+            back = pltpu.roll(packed, (LANES - 8 * t - 4) % LANES, 1)
+            TG[k, 4, row : row + 8, :] = jnp.where((lane2 < 4) | (lane2 >= 124), back, 0.0)
+
+    def gram_sums(e, k, half):
+        for row, count in GRAM_U[half]:
+            _, u = spread(TG.at[k], K, row, count)
+            UG[k, :, row : row + count, :] = u
+        for row, count in GRAM_OWN[half]:
+            _, w = spread(UG.at[k], K, row, count)
+            WG[k, :, row - LOW : row - LOW + count, :] = w[:4]
+        first = GRAM_OWN[half][0][0]
+        end = sum(GRAM_OWN[half][-1])
+
+        def pair(q, _):
+            j, _, _, held = slab_at(q)
+
+            @pl.when(held)
             def _():
-                for copy in slab_copies(k, fs.at[dx], fps.at[dx], sib):
-                    copy.start()
-
-            for half in range(2):
-                packed = PT[k, 8 * half : 8 * half + 8, :]
-                for t in range(9):
-                    row = TOP + 8 * (9 * half + t)
-                    back = pltpu.roll(packed, (LANES - 8 * t - 4) % LANES, 1)
-                    TG[k, 4, row : row + 8, :] = jnp.where((lane2 < 4) | (lane2 >= 124), back, 0.0)
-            for row, count in FULL:
-                _, u = spread(TG.at[k], K, row, count)
-                UG[k, :, row : row + count, :] = u
-            for row, count in OWN:
-                _, w = spread(UG.at[k], K, row, count)
-                WG[:, row - LOW : row - LOW + count, :] = w[:4]
-
-            def pair(q, _):
-                j, _, held = slab_at(q)
-
-                @pl.when(held)
+                sums = Sums()
+                low, high = jnp.minimum(j, k), jnp.maximum(j, k)
+                for t in range(4):
+                    tk, uk = TG[high, t, first:end, :], UG[high, t, first:end, :]
+                    wk = WG[high, t, first - LOW : end - LOW, :]
+                    tj, uj = TG[low, t, first:end, :], UG[low, t, first:end, :]
+                    sums.add(0, tj, tk)
+                    sums.add(1, tj, uk)
+                    sums.add(2, uj, uk)
+                    sums.add(3, uj, wk)
+                for i in range(4):
+                    value = jnp.sum(sums.terms[i], axis=0, keepdims=True)
+                    ROW[i, k, pl.ds(j, 1), :] = value
+                    ROW[i, j, pl.ds(k, 1), :] = value
+
+            return 0
+
+        lax.fori_loop(0, e + 1, pair, 0)
+
+    def arrive(i, _):
+        late = i >= 10
+        half = jnp.where(i < 2, i, jnp.where(late, (i - 10) // 2, (i - 2) // 4))
+        e = jnp.where(i < 2, 0, jnp.where(late, 5 + i % 2, 1 + (i - 2) % 4))
+        k, dx, same, valid = slab_at(e)
+        for h in range(2):
+            @pl.when(valid & (half == h))
+            def _():
+                @pl.when((e > 0) | (core == 0))
                 def _():
-                    sums = Sums()
-                    for t in range(4):
-                        tk, uk, wk = TG[k, t, LOW:END, :], UG[k, t, LOW:END, :], WG[t]
-                        tj, uj = TG[j, t, LOW:END, :], UG[j, t, LOW:END, :]
-                        sums.add(0, tj, tk)
-                        sums.add(1, tj, uk)
-                        sums.add(2, uj, uk)
-                        sums.add(3, uj, wk)
-                    for i in range(4):
-                        value = jnp.sum(sums.terms[i], axis=0, keepdims=True)
-                        ROW[i, k, pl.ds(j, 1), :] = value
-                        ROW[i, j, pl.ds(k, 1), :] = value
-
-                return 0
-
-            lax.fori_loop(0, e + 1, pair, 0)
+                    with jax.named_scope("b1_slabwait"):
+                        landed(half_copies(k, h, ts.at[0, h], sib))
+
+                    @pl.when(same)
+                    def _():
+                        start(half_copies(k, h, fs.at[dx, h], sib))
+
+                    do_relay, target = relay_from(e, h)
+
+                    @pl.when(do_relay)
+                    def _():
+                        start(half_copies(k, h, rs.at[0, h], target))
+
+                    unpack(k, h)
+
+                @pl.when(core == h)
+                def _():
+                    gram_sums(e, k, h)
 
         return 0
 
     phase("b1_arrive")
-    lax.fori_loop(0, 7, arrive, 0)
+    lax.fori_loop(0, 14, arrive, 0)
+
+    @pl.when(chip == 3)
+    def _():
+        landed(half_copies(below, 1, ts.at[0, 1], sib))
+        start(half_copies(below, 1, rs.at[0, 1], wrapped))
 
     phase("b2_gram")
     lane3 = lane_iota((8, 8, LANES))
@@ -478,9 +529,30 @@
     for i in range(4):
         gram = jnp.where(lane3 == 8 * i + sub3, jnp.sum(ROW[i], axis=2, keepdims=True), gram)
     gram = jnp.sum(gram, axis=1)
-    send_sums(2, jnp.concatenate([gram, jnp.zeros((8, LANES), jnp.float32)], 0))
+    GM[...] = gram
+    GR[core * 16 + me] = gram
+    pl.semaphore_wait(plane_sem, 1)
+
+    def send_gram(step, _):
+        there = lax.rem(me + step, 16)
+        place = {"lat": there // 4, "lon": there % 4}
+
+        @pl.when(step < 16)
+        def _():
+            pltpu.make_async_remote_copy(
+                GM, GR.at[core * 16 + me], gs, gr, device_id=place, device_id_type=MESH
+            ).start()
+
+        pltpu.make_async_remote_copy(
+            GM, GR.at[core * 16 + me], gs, gr, device_id={"tm": sib, **place}, device_id_type=MESH
+        ).start()
+        return 0
+
+    lax.fori_loop(1, 17, send_gram, 0)
     phase("b3_wait")
-    total = recv_sums(2)[:8]
+    box = GR.at[pl.ds(0, 31)]
+    pltpu.make_async_copy(box, box, gr).wait()
+    total = jnp.sum(GR[...], axis=0)
     phase("b4_chain")
 
     lane = lane_iota((8, LANES))
@@ -525,7 +597,7 @@
         part = slice(row, row + count)
         value = F[CG, :, part, :] * last
         for k in range(1, 8):
-            value = value + scaled(held_c[k], TG[k, :, part, :])
+            value = value + scaled(held_c[k], jnp.where(tm < k, TG[k, :, part, :], 0.0))
         V[:, part, :] = value
 
     def put(level, row, value):
@@ -546,7 +618,7 @@
             part = slice(row, row + count)
             put(0, row, scaled(psi, V[:4, part, :]) + TG[tm, :4, part, :])
 
-    _, (a, b), c = two_steps(3, X, G2, 2, write_first)
+    _, (a, b), c = two_steps(2, X, G2, 2, write_first)
     for row, count in OWN:
         part = slice(row, row + count)
         v, u, w = X[:4, part, :], U[:4, part, :], W[:4, part, :]
@@ -561,15 +633,30 @@
     phase("c9_end")
     for copy in halos:
         copy.wait_send()
-    for r in range(4):
+    for r in range(3):
         box = AR.at[r, pl.ds(0, 15)]
         pltpu.make_async_copy(box, box, ar_s.at[r]).wait()
-    each_send(lambda copy: copy.wait_send())
+    box = GR.at[pl.ds(0, 31)]
+    pltpu.make_async_copy(box, box, gs).wait()
+    own_sends(sent)
     for dx in (1, 3, 2):
         @pl.when(chip + dx <= 3)
         def _():
-            for copy in slab_copies(jnp.minimum(tm + 2 * dx, 7), fs.at[dx], fps.at[dx], sib):
-                copy.wait_send()
+            for h in range(2):
+                sent(half_copies(jnp.minimum(tm + 2 * dx, 7), h, fs.at[dx, h], sib))
+
+    @pl.when((chip == 1) | (chip == 2))
+    def _():
+        sent(half_copies(above, 0, rs.at[0, 0], below))
+
+    @pl.when(chip == 0)
+    def _():
+        sent(half_copies(jnp.minimum(tm + 6, 7), 1, rs.at[0, 1], above))
+
+    @pl.when(chip == 3)
+    def _():
+        sent(half_copies(below, 1, rs.at[0, 1], wrapped))
+
     phase(None)
 
 
@@ -592,7 +679,7 @@
             pltpu.VMEM((3, *field), f32),
             pltpu.VMEM((8, *field), f32),
             pltpu.VMEM((8, *field), f32),
-            pltpu.VMEM((4, 128, LANES), f32),
+            pltpu.VMEM((8, 4, 128, LANES), f32),
             pltpu.VMEM((4, 128, LANES), f32),
             pltpu.VMEM((4, 128, LANES), jnp.int32),
             pltpu.VMEM((3, 4, 8, LANES), f32),
@@ -602,19 +689,23 @@
             pltpu.VMEM((4, 8, LANES), f32),
             pltpu.VMEM((4, 8, LANES), f32),
             pltpu.VMEM((8, 16, LANES), f32),
-            pltpu.VMEM((4, 16, LANES), f32),
-            pltpu.VMEM((4, 16, 16, LANES), f32),
+            pltpu.VMEM((3, 16, LANES), f32),
+            pltpu.VMEM((3, 16, 16, LANES), f32),
+            pltpu.VMEM((8, LANES), f32),
+            pltpu.VMEM((32, 8, LANES), f32),
             dma((7, 4)),
             dma((10,)),
             dma((10,)),
-            dma((4,)),
-            dma((4,)),
-            dma((4,)),
-            dma((8,)),
-            dma((4,)),
-            dma((8,)),
-            dma((4,)),
-            dma((4,)),
+            dma((3,)),
+            dma((3,)),
+            dma((3, 2, 2)),
+            dma((8, 2)),
+            dma((8, 2)),
+            dma((4, 2, 2)),
+            dma((1, 2, 2)),
+            dma,
+            dma,
+            pltpu.SemaphoreType.REGULAR,
         ],
         compiler_params=pltpu.CompilerParams(
             collective_id=0, has_side_effects=True, vmem_limit_bytes=VMEM_LIMIT

time: 56.7 us -> 53.8 us (0.949); the launches traced: 55.6 us -> 53.4 us
  Pallas kernels: 54.7 us -> 52.5 us
    pallas_call x1, Pallas kernels: 54.7 us -> 52.5 us  [local(): pl.pallas_call(kernel, out_shape=jax.ShapeDtypeStruct(forcing.shape, f32)...]
where the time goes in v3:
time: 53.8 us; the launch traced here: 53.4 us
  Pallas kernels  52.5 us (98%)
  local copies, waits for them, and re-layouts  0.97 us (2%)
    pallas_call x1, Pallas kernels, local(): pl.pallas_call(kernel, out_shape=jax.ShapeDtypeStruct(forcing.shape, f32)...  52.5 us

profile of v3, /device:TPU:1, one launch (start us, length us, event | category | flops | bytes accessed | tf_op | source)
XLA Modules:
  0.0 53.4 jit_solution(2112015326584658129)
XLA Ops:
  0.0 52.5 %cycle.1 = f32[4,128,512]{2,1,0:T(8,128)S(1)} custom-call(f32[4,128,512]{2,1,0:T(8,128)} %forcing.1, f32[128,512]{1,0:T(8,128)} %depth.1, s32[128,512]{1,0:T(8,128)} %mask.1, f32[1,128,512]{2,1,0:T(8,128)} %guess.1), custom_call_target="tpu_custom_call" | custom-call | tf_op jit(solution)/shard_map/cycle/pallas_call | solution.py:667
  52.5 1.0 %copy.6 = f32[4,128,512]{2,1,0:T(8,128)} copy(f32[4,128,512]{2,1,0:T(8,128)S(1)} %cycle.1) | data formatting | bytes 2097152

commit v4 on v3

--- a/solution.py
+++ b/solution.py
@@ -14,11 +14,12 @@
 
 TILES, ROWS, LANES = 5, 160, 128
 TOP, LOW, END = 8, 16, 144
-FULL = ((8, 48), (56, 48), (104, 48))
-OWN = ((16, 64), (80, 64))
-HALVES = ((12, 68), (80, 68))
-GRAM_U = (((8, 32), (40, 36)), ((64, 48), (112, 40)))
-GRAM_OWN = (((16, 56),), ((72, 40), (112, 32)))
+FULL = tuple((row, 24) for row in range(8, 152, 24))
+OWN = tuple((row, 32) for row in range(16, 144, 32))
+HALF_ROWS = 96
+HALF = ((8, 24), (32, 24), (56, 32))
+HALF_OWN = ((16, 32), (48, 32))
+HALF_LOW, HALF_END = 16, 80
 DM, CG, G3, G2, G1, G0 = range(6)
 
 
@@ -93,7 +94,7 @@
 
 def kernel(
     forcing, depth, mask, guess, out,
-    F, K, V, X, U, W, LG, TG, UG, WG, DEP, MSK, KAP, ROW,
+    F, K, V, X, U, W, LG, GP, KH, TH, UG, TG2, TG3, TG4, DEP, MSK, KAP, ROW, CR, KQ,
     PKS, PKR, CKS, CKR, PT, MSG, AR,
     GM, GR, in_sem, hs, hr, ar_s, ar_r, ts, tr, tpr, fs, rs, gs, gr, plane_sem,
 ):
@@ -119,13 +120,12 @@
     for a in (north, south):
         for b in (west, east):
             greet({"lat": a, "lon": b})
-    for step in (4, 2, 6):
+    for step in (4, 3, 5, 2, 6, 1, 7):
         greet({"tm": lax.rem(tm + step, 8)})
     for a in (north, south):
         greet({"lat": a})
     for b in (west, east):
         greet({"lon": b})
-    greet({"tm": sib})
 
     loads = []
     own_rows = pl.ds(LOW, END - LOW)
@@ -159,11 +159,16 @@
         clear(ref)
 
     def clear_slab(i, _):
-        clear(TG.at[i])
-        ROW[:, i] = jnp.zeros((4, 8, LANES), jnp.float32)
+        ROW[:, i] = jnp.zeros((8, 8, LANES), jnp.float32)
+        CR[i] = jnp.zeros((16, LANES), jnp.float32)
         return 0
 
     lax.fori_loop(0, 8, clear_slab, 0)
+    KQ[...] = jnp.zeros((24, LANES), jnp.float32)
+    for i in range(9):
+        clear(GP.at[i])
+    for i in range(3):
+        clear(LG.at[i])
 
     phase("a2_loadwait")
     for copy in loads:
@@ -193,7 +198,7 @@
         CKS[i] = packed
 
     phase("a4_barrier")
-    pl.semaphore_wait(barrier, 12)
+    pl.semaphore_wait(barrier, 15)
 
     halos = []
 
@@ -292,6 +297,35 @@
             sums.add(3, lg[:4], llg[:4])
         for i in range(4):
             KAP[slot, i] = sums.terms[i]
+
+    def power(src, dst):
+        for row, count in FULL:
+            dst[:, row : row + count, :] = spread(src, K, row, count)[1]
+
+    def line(acc):
+        return jnp.sum(acc, axis=0, keepdims=True)
+
+    def own_sum(a, b):
+        return line(fold(a[:4, LOW:END, :] * b[:4, LOW:END, :]))
+
+    g3_powers = [F.at[G3], LG.at[0]] + [GP.at[i] for i in range(5)]
+    g2_powers = [F.at[G2], LG.at[2]] + [GP.at[i] for i in range(5, 9)]
+
+    def powers_of_g3():
+        for src, dst in zip(g3_powers[1:], g3_powers[2:]):
+            power(src, dst)
+
+    def powers_of_g2():
+        prepare(G2, 2)
+        for src, dst in zip(g2_powers[1:], g2_powers[2:]):
+            power(src, dst)
+        for i in range(4):
+            KQ[i : i + 1, :] = line(KAP[0, i])
+            KQ[11 + i : 12 + i, :] = line(KAP[2, i])
+        KQ[4:5, :] = own_sum(g3_powers[2], g3_powers[2])
+        KQ[5:6, :] = own_sum(g3_powers[2], g3_powers[3])
+        for i in range(5):
+            KQ[6 + i : 7 + i, :] = own_sum(g2_powers[0], g3_powers[i])
 
     def two_steps(r, v_ref, field, slot, between):
         phase(f"r{r}_moments")
@@ -352,6 +386,10 @@
         for copy in halos[8:]:
             copy.wait_recv()
         prepare(G1, 1)
+        powers_of_g3()
+        rows = pl.ds(pl.multiple_of(8 + 64 * core, 8), 80)
+        for i in range(4):
+            KH[i, :, 8:88, :] = K[i, :, rows, :]
 
     m_start, _, c = two_steps(0, F.at[CG], G3, 0, rest_of_halo)
     for row, count in FULL:
@@ -364,29 +402,31 @@
     psi = m_start[0] / (m_start[0] + 4.0 * m_start[1] + EPS)
     drop = psi * (last - 1.0)
 
-    _, _, c = two_steps(1, X, G1, 1, lambda: prepare(G2, 2))
-    for row, count in FULL:
-        part = slice(row, row + count)
-        TG[tm, :, part, :] = (
-            scaled(c[0], X[:, part, :]) + scaled(c[1], U[:, part, :]) + scaled(c[2], W[:, part, :])
-            + scaled(c[3], F[G1, :, part, :]) + scaled(c[4], LG[1, :, part, :]) + F[G0, :, part, :]
-            + scaled(drop, F[CG, :, part, :])
-        )
+    _, _, c = two_steps(1, X, G1, 1, powers_of_g2)
+    for h in range(2):
+        for row, count in HALF:
+            part = slice(64 * h + row, 64 * h + row + count)
+            TH[h, tm, :, row : row + count, :] = (
+                scaled(c[0], X[:, part, :]) + scaled(c[1], U[:, part, :])
+                + scaled(c[2], W[:, part, :]) + scaled(c[3], F[G1, :, part, :])
+                + scaled(c[4], LG[1, :, part, :]) + F[G0, :, part, :]
+                + scaled(drop, F[CG, :, part, :])
+            )
 
     phase("b0_gather")
     lane2 = lane_iota((8, LANES))
-    for half in range(2):
+    for h in range(2):
         packed = jnp.zeros((8, LANES), jnp.float32)
-        for t in range(9):
-            row = TOP + 8 * (9 * half + t)
+        for t in range(10):
+            row = 8 + 8 * t
             here = (lane2 >= 8 * t) & (lane2 < 8 * t + 8)
-            packed = jnp.where(here, pltpu.roll(TG[tm, 4, row : row + 8, :], 8 * t + 4, 1), packed)
-        PT[tm, 8 * half : 8 * half + 8, :] = packed
+            edge = pltpu.roll(TH[h, tm, 4, row : row + 8, :], 8 * t + 4, 1)
+            packed = jnp.where(here, edge, packed)
+        PT[tm, h] = packed
 
     def half_copies(k, h, sems, target):
-        row, count = HALVES[h]
-        main = TG.at[k, pl.ds(0, 4), pl.ds(row, count), :]
-        pack = PT.at[k, pl.ds(8 * h, 8), :]
+        main = TH.at[h, k, pl.ds(0, 4), pl.ds(12, 72), :]
+        pack = PT.at[k, h]
         return [
             pltpu.make_async_remote_copy(
                 ref, ref, sems.at[i], recv.at[k, h], device_id={"tm": target}, device_id_type=MESH
@@ -394,9 +434,6 @@
             for i, (ref, recv) in enumerate(((main, tr), (pack, tpr)))
         ]
 
-    below, above = jnp.maximum(tm - 2, 0), jnp.minimum(tm + 2, 7)
-    wrapped = lax.rem(tm + 2, 8)
-
     def own_sends(act):
         for h in range(2):
             @pl.when(core == 1)
@@ -405,16 +442,16 @@
 
             @pl.when(chip == 3)
             def _():
-                act(half_copies(tm, h, ts.at[1, h], wrapped))
+                act(half_copies(tm, h, ts.at[1, h], h))
 
             @pl.when(chip >= 1)
             def _():
-                act(half_copies(tm, h, ts.at[2, h], below))
+                act(half_copies(tm, h, ts.at[2, h], jnp.maximum(2 * chip - 2 + h, 0)))
 
             if h == 1:
                 @pl.when(chip == 2)
                 def _():
-                    act(half_copies(tm, h, ts.at[1, h], above))
+                    act(half_copies(tm, h, ts.at[1, h], 7))
 
     def start(copies):
         for copy in copies:
@@ -432,32 +469,26 @@
 
     def slab_at(e):
         dx = jnp.where(e >= 5, 2, jnp.where(e % 2 == 1, 1, 3))
-        same = (e == 1) | (e == 2) | (e == 5)
-        k = jnp.where(e == 0, 2 * chip + 1, jnp.where(same, tm, sib) + 2 * dx)
+        odd = jnp.where((e == 1) | (e == 2) | (e == 5), 1, 0)
+        k = jnp.where(e == 0, 2 * chip + 1, 2 * (chip + dx) + odd)
         valid = (e == 0) | (chip + dx <= 3)
-        return jnp.minimum(k, 7), dx, same, valid
-
-    def relay_from(e, h):
-        if h == 0:
-            return (e == 1) & ((chip == 1) | (chip == 2)), below
-        return (e == 2) & (chip == 0), above
+        return jnp.minimum(k, 7), dx, odd, valid
 
     def unpack(k, h):
-        packed = PT[k, 8 * h : 8 * h + 8, :]
-        for t in range(9):
-            row = TOP + 8 * (9 * h + t)
+        packed = PT[k, h]
+        for t in range(10):
             back = pltpu.roll(packed, (LANES - 8 * t - 4) % LANES, 1)
-            TG[k, 4, row : row + 8, :] = jnp.where((lane2 < 4) | (lane2 >= 124), back, 0.0)
-
-    def gram_sums(e, k, half):
-        for row, count in GRAM_U[half]:
-            _, u = spread(TG.at[k], K, row, count)
-            UG[k, :, row : row + count, :] = u
-        for row, count in GRAM_OWN[half]:
-            _, w = spread(UG.at[k], K, row, count)
-            WG[k, :, row - LOW : row - LOW + count, :] = w[:4]
-        first = GRAM_OWN[half][0][0]
-        end = sum(GRAM_OWN[half][-1])
+            back = jnp.where((lane2 < 4) | (lane2 >= 124), back, 0.0)
+            TH[h, k, 4, 8 + 8 * t : 16 + 8 * t, :] = back
+
+    def gram_sums(e, k):
+        refs = [TH.at[core, k], UG.at[k], TG2.at[k], TG3.at[k]]
+        for src, dst in zip(refs, refs[1:]):
+            for row, count in HALF:
+                dst[:, row : row + count, :] = spread(src, KH, row, count)[1]
+        for row, count in HALF_OWN:
+            last_power = spread(refs[3], KH, row, count)[1]
+            TG4[k, :, row - HALF_LOW : row - HALF_LOW + count, :] = last_power[:4]
 
         def pair(q, _):
             j, _, _, held = slab_at(q)
@@ -467,15 +498,16 @@
                 sums = Sums()
                 low, high = jnp.minimum(j, k), jnp.maximum(j, k)
                 for t in range(4):
-                    tk, uk = TG[high, t, first:end, :], UG[high, t, first:end, :]
-                    wk = WG[high, t, first - LOW : end - LOW, :]
-                    tj, uj = TG[low, t, first:end, :], UG[low, t, first:end, :]
-                    sums.add(0, tj, tk)
-                    sums.add(1, tj, uk)
-                    sums.add(2, uj, uk)
-                    sums.add(3, uj, wk)
-                for i in range(4):
-                    value = jnp.sum(sums.terms[i], axis=0, keepdims=True)
+                    a, b = (
+                        [TH[core, s, t, HALF_LOW:HALF_END, :]]
+                        + [ref[s, t, HALF_LOW:HALF_END, :] for ref in (UG, TG2, TG3)]
+                        for s in (low, high)
+                    )
+                    b.append(TG4[high, t])
+                    for i in range(8):
+                        sums.add(i, a[i // 2], b[(i + 1) // 2])
+                for i in range(8):
+                    value = line(sums.terms[i])
                     ROW[i, k, pl.ds(j, 1), :] = value
                     ROW[i, j, pl.ds(k, 1), :] = value
 
@@ -483,52 +515,104 @@
 
         lax.fori_loop(0, e + 1, pair, 0)
 
+    def cross_sums(k, h):
+        sums = Sums()
+        rows = pl.ds(pl.multiple_of(HALF_LOW + 64 * h, 8), HALF_END - HALF_LOW)
+        for t in range(4):
+            value = TH[h, k, t, HALF_LOW:HALF_END, :]
+            for i, ref in enumerate(g3_powers + g2_powers):
+                sums.add(i, value, ref[t, rows, :])
+        for i in range(13):
+            CR[k, i : i + 1, :] = CR[k, i : i + 1, :] + line(sums.terms[i])
+
+    def first_hand(e):
+        k, dx, odd, valid = slab_at(e)
+
+        @pl.when(valid)
+        def _():
+            @pl.when((e > 0) | (core == 0))
+            def _():
+                with jax.named_scope("b1_slabwait"):
+                    landed(half_copies(k, core, ts.at[0, 0], sib))
+
+            @pl.when((dx == 1) & (core == 0) & ((chip == 1) | (chip == 2)) & (e > 0))
+            def _():
+                start(half_copies(k, 0, rs.at[odd], jnp.maximum(tm - 2, 0)))
+
+            @pl.when((dx == 3) & (core == 1) & (chip == 0) & (e > 0))
+            def _():
+                start(half_copies(k, 1, rs.at[odd], 3))
+
+            @pl.when(e > 0)
+            def _():
+                start(half_copies(k, core, fs.at[e], sib))
+
+            @pl.when(k > tm)
+            def _():
+                unpack(k, core)
+
+            gram_sums(e, k)
+
+            @pl.when(k > tm)
+            def _():
+                cross_sums(k, core)
+
+    def second_hand(e):
+        k, _, _, valid = slab_at(e)
+
+        @pl.when(valid & (k > tm))
+        def _():
+            with jax.named_scope("b1_sibwait"):
+                landed(half_copies(k, 1 - core, ts.at[0, 0], sib))
+            unpack(k, 1 - core)
+            cross_sums(k, 1 - core)
+
     def arrive(i, _):
-        late = i >= 10
-        half = jnp.where(i < 2, i, jnp.where(late, (i - 10) // 2, (i - 2) // 4))
-        e = jnp.where(i < 2, 0, jnp.where(late, 5 + i % 2, 1 + (i - 2) % 4))
-        k, dx, same, valid = slab_at(e)
-        for h in range(2):
-            @pl.when(valid & (half == h))
-            def _():
-                @pl.when((e > 0) | (core == 0))
-                def _():
-                    with jax.named_scope("b1_slabwait"):
-                        landed(half_copies(k, h, ts.at[0, h], sib))
-
-                    @pl.when(same)
-                    def _():
-                        start(half_copies(k, h, fs.at[dx, h], sib))
-
-                    do_relay, target = relay_from(e, h)
-
-                    @pl.when(do_relay)
-                    def _():
-                        start(half_copies(k, h, rs.at[0, h], target))
-
-                    unpack(k, h)
-
-                @pl.when(core == h)
-                def _():
-                    gram_sums(e, k, h)
+        @pl.when(i < 7)
+        def _():
+            first_hand(jnp.minimum(i, 6))
+
+        @pl.when(i >= 3)
+        def _():
+            second_hand(jnp.maximum(i - 3, 0))
 
         return 0
 
+    @pl.when(tm == 7)
+    def _():
+        refs = [F.at[CG], U, W, V, X]
+        for src, dst in zip(refs, refs[1:]):
+            power(src, dst)
+        for i in range(8):
+            KQ[16 + i : 17 + i, :] = own_sum(refs[i // 2], refs[(i + 1) // 2])
+        for i, ref in enumerate(g3_powers + g2_powers):
+            CR[0, i : i + 1, :] = own_sum(refs[0], ref)
+
+    @pl.when(tm == 7)
+    def _():
+        for odd in (1, 0):
+            landed(half_copies(4 + odd, 1, ts.at[0, 0], sib))
+            start(half_copies(4 + odd, 1, rs.at[odd], 1))
+
     phase("b1_arrive")
-    lax.fori_loop(0, 14, arrive, 0)
-
-    @pl.when(chip == 3)
-    def _():
-        landed(half_copies(below, 1, ts.at[0, 1], sib))
-        start(half_copies(below, 1, rs.at[0, 1], wrapped))
+    lax.fori_loop(0, 10, arrive, 0)
 
     phase("b2_gram")
     lane3 = lane_iota((8, 8, LANES))
     sub3 = lax.broadcasted_iota(jnp.int32, (8, 8, LANES), 1)
     gram = jnp.zeros((8, 8, LANES), jnp.float32)
-    for i in range(4):
+    for i in range(8):
         gram = jnp.where(lane3 == 8 * i + sub3, jnp.sum(ROW[i], axis=2, keepdims=True), gram)
     gram = jnp.sum(gram, axis=1)
+    lane4 = lane_iota((8, 16, LANES))
+    sub4 = lax.broadcasted_iota(jnp.int32, (8, 16, LANES), 1)
+    cross = jnp.where(lane4 == 64 + sub4, jnp.sum(CR[...], axis=2, keepdims=True), 0.0)
+    gram = gram + jnp.sum(cross, axis=1)
+    lane5 = lane_iota((24, LANES))
+    sub5 = lax.broadcasted_iota(jnp.int32, (24, LANES), 0)
+    own = jnp.where(lane5 == 80 + sub5, jnp.sum(KQ[...], axis=1, keepdims=True), 0.0)
+    own = jnp.sum(own, axis=0, keepdims=True)
+    gram = gram + jnp.where(lax.broadcasted_iota(jnp.int32, (8, LANES), 0) == 0, own, 0.0)
     GM[...] = gram
     GR[core * 16 + me] = gram
     pl.semaphore_wait(plane_sem, 1)
@@ -553,18 +637,19 @@
     box = GR.at[pl.ds(0, 31)]
     pltpu.make_async_copy(box, box, gr).wait()
     total = jnp.sum(GR[...], axis=0)
+    plane = jnp.sum(GR[pl.ds(core * 16, 16)], axis=0)
     phase("b4_chain")
 
     lane = lane_iota((8, LANES))
-    table = [
-        [
-            None if j == 0 else jnp.broadcast_to(
-                jnp.sum(jnp.where(lane == 8 * i + j, total, 0.0), axis=1, keepdims=True), (8, LANES)
-            )
-            for j in range(8)
-        ]
-        for i in range(4)
-    ]
+
+    def column(source, i):
+        picked = jnp.sum(jnp.where(lane == i, source, 0.0), axis=1, keepdims=True)
+        return jnp.broadcast_to(picked, (8, LANES))
+
+    table = [[None if j == 0 else column(total, 8 * i + j) for j in range(8)] for i in range(8)]
+    with_g = [column(plane, 64 + i) for i in range(13)]
+    first_row = [column(plane, 80 + i)[0:1, :] for i in range(24)]
+    k33, k32, k22 = first_row[:6], first_row[6:11], first_row[11:15]
 
     def entry(i, k, j):
         return table[i][j][k : k + 1, :]
@@ -572,90 +657,101 @@
     one = jnp.ones((1, LANES), jnp.float32)
     zero = jnp.zeros((1, LANES), jnp.float32)
     coefs = {7: one}
-    quad = [entry(i, 7, 7) for i in range(4)]
-    cross = [{j: entry(i, 7, j) for j in range(1, 7)} for i in range(4)]
+    quad = [entry(i, 7, 7) for i in range(8)]
+    cross = [{j: entry(i, 7, j) for j in range(1, 7)} for i in range(8)]
+    mixed = [x[7:8, :] for x in with_g]
     is_last = jnp.full((1, LANES), tm == 7)
     held_c = {k: zero for k in range(1, 8)}
-    held_q = [m_start[i] for i in range(4)]
+    held_q = first_row[16:24]
+    held_m = [x[0:1, :] for x in with_g]
     for t in range(7, 0, -1):
         if t < 7:
             psi_t = quad[0] / (quad[0] + 4.0 * quad[1] + EPS)
             quad = [
                 psi_t * psi_t * quad[i] + 2.0 * psi_t * cross[i][t] + entry(i, t, t)
-                for i in range(4)
+                for i in range(8)
             ]
-            cross = [{j: psi_t * cross[i][j] + entry(i, t, j) for j in range(1, t)} for i in range(4)]
+            cross = [{j: psi_t * cross[i][j] + entry(i, t, j) for j in range(1, t)} for i in range(8)]
+            mixed = [psi_t * x + y[t : t + 1, :] for x, y in zip(mixed, with_g)]
             coefs = {k: psi_t * x for k, x in coefs.items()}
             coefs[t] = one
         now = jnp.full((1, LANES), tm + 1 == t)
         for k in coefs:
             held_c[k] = jnp.where(now, coefs[k], held_c[k])
-        held_q = [jnp.where(now, quad[i], held_q[i]) for i in range(4)]
+        held_q = [jnp.where(now, quad[i], held_q[i]) for i in range(8)]
+        held_m = [jnp.where(now, mixed[i], held_m[i]) for i in range(13)]
     psi = held_q[0] / (held_q[0] + 4.0 * held_q[1] + EPS)
     psi = jnp.where(is_last, 0.0, psi)
     for row, count in FULL:
         part = slice(row, row + count)
         value = F[CG, :, part, :] * last
         for k in range(1, 8):
-            value = value + scaled(held_c[k], jnp.where(tm < k, TG[k, :, part, :], 0.0))
+            slab = TH[row // 80, k, :, row - 64 * (row // 80) : row - 64 * (row // 80) + count, :]
+            value = value + scaled(held_c[k], jnp.where(tm < k, slab, 0.0))
         V[:, part, :] = value
 
     def put(level, row, value):
         for t in range(4):
             out[level, row - LOW : row - LOW + value.shape[1], cols(t)] = value[t]
 
+    def next_moments(a, b, m, n, k, count):
+        return [
+            jnp.maximum(
+                a * a * m[i] + 2.0 * a * b * m[i + 1] + b * b * m[i + 2]
+                + 2.0 * (a * n[i] + b * n[i + 1]) + k[i],
+                0.0,
+            )
+            for i in range(count)
+        ]
+
+    a1, b1 = fine_coefs(held_q)
+    m1 = next_moments(a1, b1, held_q, held_m[:7], k33, 6)
+    n1 = [a1 * held_m[7 + i] + b1 * held_m[8 + i] + k32[i] for i in range(5)]
+    a2, b2 = fine_coefs(m1)
+    m2 = next_moments(a2, b2, m1, n1, k22, 4)
+    a3, b3 = fine_coefs(m2)
     phase("c0_correct")
-    a, b = fine_coefs(held_q)
     for row, count in FULL:
         part = slice(row, row + count)
         v, u = spread(V, K, row, count)
-        value = scaled(a, v) + scaled(b, u) + F[G3, :, part, :]
+        value = scaled(a1, v) + scaled(b1, u) + F[G3, :, part, :]
         X[:, part, :] = value
         put(3, max(row, LOW), own_part(value, row, count))
-
-    def write_first():
-        for row, count in OWN:
-            part = slice(row, row + count)
-            put(0, row, scaled(psi, V[:4, part, :]) + TG[tm, :4, part, :])
-
-    _, (a, b), c = two_steps(2, X, G2, 2, write_first)
+    for row, count in FULL:
+        part = slice(row, row + count)
+        v, u = spread(X, K, row, count)
+        value = scaled(a2, v) + scaled(b2, u) + F[G2, :, part, :]
+        W[:, part, :] = value
+        put(2, max(row, LOW), own_part(value, row, count))
     for row, count in OWN:
         part = slice(row, row + count)
-        v, u, w = X[:4, part, :], U[:4, part, :], W[:4, part, :]
-        g = F[G2, :4, part, :]
-        put(2, row, scaled(a, v) + scaled(b, u) + g)
-        last_value = (
-            scaled(c[0], v) + scaled(c[1], u) + scaled(c[2], w) + scaled(c[3], g)
-            + scaled(c[4], LG[2, :4, part, :]) + F[G1, :4, part, :]
-        )
-        put(1, row, last_value)
+        v, u = spread(W, K, row, count)
+        put(1, row, scaled(a3, v[:4]) + scaled(b3, u[:4]) + F[G1, :4, part, :])
+        first = row - 64 * (row // 80)
+        put(0, row, scaled(psi, V[:4, part, :]) + TH[row // 80, tm, :4, first : first + count, :])
 
     phase("c9_end")
     for copy in halos:
         copy.wait_send()
-    for r in range(3):
+    for r in range(2):
         box = AR.at[r, pl.ds(0, 15)]
         pltpu.make_async_copy(box, box, ar_s.at[r]).wait()
     box = GR.at[pl.ds(0, 31)]
     pltpu.make_async_copy(box, box, gs).wait()
     own_sends(sent)
-    for dx in (1, 3, 2):
-        @pl.when(chip + dx <= 3)
+    for e in range(1, 7):
+        k, _, _, valid = slab_at(e)
+
+        @pl.when(valid)
         def _():
-            for h in range(2):
-                sent(half_copies(jnp.minimum(tm + 2 * dx, 7), h, fs.at[dx, h], sib))
-
-    @pl.when((chip == 1) | (chip == 2))
+            sent(half_copies(k, core, fs.at[e], sib))
+
+    relays = ((core == 0) & ((chip == 1) | (chip == 2))) | ((core == 1) & ((chip == 0) | (chip == 3)))
+
+    @pl.when(relays)
     def _():
-        sent(half_copies(above, 0, rs.at[0, 0], below))
-
-    @pl.when(chip == 0)
-    def _():
-        sent(half_copies(jnp.minimum(tm + 6, 7), 1, rs.at[0, 1], above))
-
-    @pl.when(chip == 3)
-    def _():
-        sent(half_copies(below, 1, rs.at[0, 1], wrapped))
+        for odd in range(2):
+            sent(half_copies(0, core, rs.at[odd], sib))
 
     phase(None)
 
@@ -663,6 +759,7 @@
 def local(forcing, depth, mask, guess):
     f32 = jnp.float32
     field = (TILES, ROWS, LANES)
+    half = (TILES, HALF_ROWS, LANES)
     dma = pltpu.SemaphoreType.DMA
     return pl.pallas_call(
         kernel,
@@ -677,32 +774,38 @@
             pltpu.VMEM(field, f32),
             pltpu.VMEM(field, f32),
             pltpu.VMEM((3, *field), f32),
-            pltpu.VMEM((8, *field), f32),
-            pltpu.VMEM((8, *field), f32),
-            pltpu.VMEM((8, 4, 128, LANES), f32),
+            pltpu.VMEM((9, *field), f32),
+            pltpu.VMEM((4, *half), f32),
+            pltpu.VMEM((2, 8, *half), f32),
+            pltpu.VMEM((8, *half), f32),
+            pltpu.VMEM((8, *half), f32),
+            pltpu.VMEM((8, *half), f32),
+            pltpu.VMEM((8, 4, 64, LANES), f32),
             pltpu.VMEM((4, 128, LANES), f32),
             pltpu.VMEM((4, 128, LANES), jnp.int32),
             pltpu.VMEM((3, 4, 8, LANES), f32),
-            pltpu.VMEM((4, 8, 8, LANES), f32),
+            pltpu.VMEM((8, 8, 8, LANES), f32),
+            pltpu.VMEM((8, 16, LANES), f32),
+            pltpu.VMEM((24, LANES), f32),
             pltpu.VMEM((2, 6, 8, LANES), f32),
             pltpu.VMEM((2, 6, 8, LANES), f32),
             pltpu.VMEM((4, 8, LANES), f32),
             pltpu.VMEM((4, 8, LANES), f32),
-            pltpu.VMEM((8, 16, LANES), f32),
-            pltpu.VMEM((3, 16, LANES), f32),
-            pltpu.VMEM((3, 16, 16, LANES), f32),
+            pltpu.VMEM((8, 2, 8, LANES), f32),
+            pltpu.VMEM((2, 16, LANES), f32),
+            pltpu.VMEM((2, 16, 16, LANES), f32),
             pltpu.VMEM((8, LANES), f32),
             pltpu.VMEM((32, 8, LANES), f32),
             dma((7, 4)),
             dma((10,)),
             dma((10,)),
-            dma((3,)),
-            dma((3,)),
+            dma((2,)),
+            dma((2,)),
             dma((3, 2, 2)),
             dma((8, 2)),
             dma((8, 2)),
-            dma((4, 2, 2)),
-            dma((1, 2, 2)),
+            dma((7, 2)),
+            dma((2, 2)),
             dma,
             dma,
             pltpu.SemaphoreType.REGULAR,

time: 53.8 us -> 47.6 us (0.88)
  Pallas kernels: 52.5 us -> 46.4 us
    pallas_call x1, Pallas kernels: 52.5 us -> 46.4 us  [local(): pl.pallas_call(kernel, out_shape=jax.ShapeDtypeStruct(forcing.shape, f32)...]
where the time goes in v4:
time: 47.6 us; the launch traced here: 47.4 us
  Pallas kernels  46.4 us (97%)
  local copies, waits for them, and re-layouts  0.97 us (2%)
    pallas_call x1, Pallas kernels, local(): pl.pallas_call(kernel, out_shape=jax.ShapeDtypeStruct(forcing.shape, f32)...  46.4 us
    unnamed x1, local copies, waits for them, and re-layouts  0.97 us

profile of v4, /device:TPU:1, one launch (start us, length us, event | category | flops | bytes accessed | tf_op | source)
XLA Modules:
  0.0 47.4 jit_solution(4100859225894147811)
XLA Ops:
  0.0 46.4 %cycle.1 = f32[4,128,512]{2,1,0:T(8,128)S(1)} custom-call(f32[4,128,512]{2,1,0:T(8,128)} %forcing.1, f32[128,512]{1,0:T(8,128)} %depth.1, s32[128,512]{1,0:T(8,128)} %mask.1, f32[1,128,512]{2,1,0:T(8,128)} %guess.1), custom_call_target="tpu_custom_call" | custom-call | tf_op jit(solution)/shard_map/cycle/pallas_call | solution.py:764
  46.4 1.0 %copy.6 = f32[4,128,512]{2,1,0:T(8,128)} copy(f32[4,128,512]{2,1,0:T(8,128)S(1)} %cycle.1) | data formatting | bytes 2097152

commit v5 on v4

--- a/solution.py
+++ b/solution.py
@@ -96,7 +96,7 @@
     forcing, depth, mask, guess, out,
     F, K, V, X, U, W, LG, GP, KH, TH, UG, TG2, TG3, TG4, DEP, MSK, KAP, ROW, CR, KQ,
     PKS, PKR, CKS, CKR, PT, MSG, AR,
-    GM, GR, in_sem, hs, hr, ar_s, ar_r, ts, tr, tpr, fs, rs, gs, gr, plane_sem,
+    GM, GR, BOX, in_sem, hs, hr, ar_s, ar_r, ts, tr, fs, rs, gs, gr, plane_sem,
 ):
     phase = Phase()
     phase("a0_load")
@@ -127,22 +127,19 @@
     for b in (west, east):
         greet({"lon": b})
 
-    loads = []
     own_rows = pl.ds(LOW, END - LOW)
 
-    def load(src, dst, field, c):
-        copy = pltpu.make_async_copy(src, dst, in_sem.at[field, c])
-        copy.start()
-        loads.append(copy)
-
     for c in range(4):
-        load(depth.at[:, cols(c)], DEP.at[c], 0, c)
-        load(mask.at[:, cols(c)], MSK.at[c], 1, c)
-    for c in range(4):
-        load(guess.at[0, :, cols(c)], F.at[CG, c, own_rows, :], 2, c)
+        pltpu.make_async_copy(depth.at[:, cols(c)], DEP.at[c], in_sem.at[0]).start()
+        pltpu.make_async_copy(mask.at[:, cols(c)], MSK.at[c], in_sem.at[1]).start()
+        pltpu.make_async_copy(
+            guess.at[0, :, cols(c)], F.at[CG, c, own_rows, :], in_sem.at[2]
+        ).start()
     for field, level in ((G3, 3), (G2, 2), (G1, 1), (G0, 0)):
         for c in range(4):
-            load(forcing.at[level, :, cols(c)], F.at[field, c, own_rows, :], 3 + level, c)
+            pltpu.make_async_copy(
+                forcing.at[level, :, cols(c)], F.at[field, c, own_rows, :], in_sem.at[2]
+            ).start()
 
     phase("a1_clear")
     def clear(ref):
@@ -171,8 +168,9 @@
         clear(LG.at[i])
 
     phase("a2_loadwait")
-    for copy in loads:
-        copy.wait()
+    fields = F.at[pl.ds(1, 5), pl.ds(0, 4), own_rows, :]
+    for i, ref in enumerate((DEP, MSK, fields)):
+        pltpu.make_async_copy(ref, ref, in_sem.at[i]).wait()
     for c in range(4):
         F[DM, c, LOW:END, :] = jnp.where(MSK[c] > 0, DEP[c], 0.0)
 
@@ -200,21 +198,22 @@
     phase("a4_barrier")
     pl.semaphore_wait(barrier, 15)
 
-    halos = []
 
     def push(src, dst, i, target):
-        copy = pltpu.make_async_remote_copy(
-            src, dst, hs.at[i], hr.at[i], device_id=target, device_id_type=MESH
-        )
-        copy.start()
-        halos.append(copy)
+        pltpu.make_async_remote_copy(
+            src, dst, hs, hr.at[i], device_id=target, device_id_type=MESH
+        ).start()
+
+    def wait_rows(sem, count):
+        box = BOX.at[pl.ds(0, count)]
+        pltpu.make_async_copy(box, box, sem).wait()
 
     targets = ((south, east), (south, west), (north, east), (north, west))
     for i, (a, b) in enumerate(targets):
-        push(CKS.at[i], CKR.at[i], i, {"lat": a, "lon": b})
-    push(PKS.at[0], PKR.at[0], 4, {"lon": east})
-    push(PKS.at[1], PKR.at[1], 5, {"lon": west})
-    for i, first in ((6, 0), (8, 3)):
+        push(CKS.at[i], CKR.at[i], 0, {"lat": a, "lon": b})
+    push(PKS.at[0], PKR.at[0], 0, {"lon": east})
+    push(PKS.at[1], PKR.at[1], 0, {"lon": west})
+    for i, first in ((0, 0), (1, 3)):
         group = pl.ds(first, 3)
         push(
             F.at[group, pl.ds(0, 4), pl.ds(136, 8), :],
@@ -224,11 +223,10 @@
         push(
             F.at[group, pl.ds(0, 4), pl.ds(16, 8), :],
             F.at[group, pl.ds(0, 4), pl.ds(144, 8), :],
-            i + 1, {"lat": north},
+            i, {"lat": north},
         )
     phase("a5_halowait")
-    for copy in halos[:8]:
-        copy.wait_recv()
+    wait_rows(hr.at[0], 4 * 8 + 2 * 48 + 2 * 96)
 
     pl.semaphore_signal(plane_sem, inc=1, device_id={"tm": sib}, device_id_type=MESH)
     phase("a6_unpack")
@@ -257,31 +255,39 @@
                 (d > 0.0) & (other > 0.0), 1.5 * (d + other), 0.0
             )
 
-    def send_sums(r, message):
-        MSG[r] = message
-        AR[r, me] = message
-
-        def one(step, _):
-            there = lax.rem(me + step, 16)
-            pltpu.make_async_remote_copy(
-                MSG.at[r], AR.at[r, me], ar_s.at[r], ar_r.at[r],
-                device_id={"lat": there // 4, "lon": there % 4}, device_id_type=MESH,
-            ).start()
-            return 0
-
-        lax.fori_loop(1, 16, one, 0)
-
-    def recv_sums(r):
-        box = AR.at[r, pl.ds(0, 15)]
-        pltpu.make_async_copy(box, box, ar_r.at[r]).wait()
-        return jnp.sum(AR[r], axis=0)
-
-    def rows_of(accs):
+    far_first = sorted(
+        ((a, b) for a in range(4) for b in range(4) if (a, b) != (0, 0)),
+        key=lambda ab: -(min(ab[0], 4 - ab[0]) + min(ab[1], 4 - ab[1])),
+    )
+
+    def plane_peer(a, b):
+        return {"lat": lax.rem(lat + a, 4), "lon": lax.rem(lon + b, 4)}
+
+    def diagonal(x, count):
+        shape = (count, LANES)
+        here = lane_iota(shape) == lax.broadcasted_iota(jnp.int32, shape, 0)
+        picked = jnp.where(here, jnp.broadcast_to(x, shape), 0.0)
+        return jnp.broadcast_to(jnp.sum(picked, axis=1, keepdims=True), shape)
+
+    def send_sums(r, accs):
         row = lax.broadcasted_iota(jnp.int32, (16, LANES), 0)
         stacked = jnp.zeros((16, LANES), jnp.float32)
         for i, acc in enumerate(accs):
             stacked = jnp.where(row == i, jnp.sum(acc, axis=0, keepdims=True), stacked)
-        return jnp.broadcast_to(jnp.sum(stacked, axis=1, keepdims=True), (16, LANES))
+        stacked = jnp.broadcast_to(jnp.sum(stacked, axis=1, keepdims=True), (16, LANES))
+        message = jnp.where(lane_iota((16, LANES)) == row, stacked, 0.0)
+        message = jnp.sum(message, axis=0, keepdims=True)
+        MSG[r, 0:1, :] = message
+        AR[r, pl.ds(me, 1), :] = message
+        for a, b in far_first:
+            pltpu.make_async_remote_copy(
+                MSG.at[r, pl.ds(0, 1)], AR.at[r, pl.ds(me, 1)], ar_s.at[r], ar_r.at[r],
+                device_id=plane_peer(a, b), device_id_type=MESH,
+            ).start()
+
+    def recv_sums(r):
+        wait_rows(ar_r.at[r], 15)
+        return diagonal(jnp.sum(AR[r], axis=0, keepdims=True), 16)
 
     def prepare(field, slot):
         sums = Sums()
@@ -356,7 +362,7 @@
             sums.add("n4", lw[:4], lg)
         names = ["m0", "m1", "m2", "m3", "m4", "m5", "n0", "n1", "n2", "n3", "n4"]
         accs = [sums.terms[n] for n in names] + [KAP[slot, i] for i in range(4)]
-        send_sums(r, rows_of(accs))
+        send_sums(r, accs)
         phase(f"r{r}_between")
         between()
         phase(f"r{r}_wait")
@@ -383,8 +389,7 @@
     prepare(G3, 0)
 
     def rest_of_halo():
-        for copy in halos[8:]:
-            copy.wait_recv()
+        wait_rows(hr.at[1], 2 * 96)
         prepare(G1, 1)
         powers_of_g3()
         rows = pl.ds(pl.multiple_of(8 + 64 * core, 8), 80)
@@ -424,52 +429,49 @@
             packed = jnp.where(here, edge, packed)
         PT[tm, h] = packed
 
-    def half_copies(k, h, sems, target):
+    def half_copies(k, h, sem, target):
         main = TH.at[h, k, pl.ds(0, 4), pl.ds(12, 72), :]
-        pack = PT.at[k, h]
         return [
             pltpu.make_async_remote_copy(
-                ref, ref, sems.at[i], recv.at[k, h], device_id={"tm": target}, device_id_type=MESH
+                ref, ref, sem, tr.at[k, h], device_id={"tm": target}, device_id_type=MESH
             )
-            for i, (ref, recv) in enumerate(((main, tr), (pack, tpr)))
+            for ref in (main, PT.at[k, h])
         ]
+
+    def start(copies):
+        for copy in copies:
+            copy.start()
+
+    def sent(sem):
+        wait_rows(sem, 4 * 72 + 8)
+
+    def landed(k, h):
+        wait_rows(tr.at[k, h], 4 * 72 + 8)
 
     def own_sends(act):
         for h in range(2):
             @pl.when(core == 1)
             def _():
-                act(half_copies(tm, h, ts.at[0, h], sib))
+                act(h, ts.at[0, h], sib)
 
             @pl.when(chip == 3)
             def _():
-                act(half_copies(tm, h, ts.at[1, h], h))
+                act(h, ts.at[1, h], h)
 
             @pl.when(chip >= 1)
             def _():
-                act(half_copies(tm, h, ts.at[2, h], jnp.maximum(2 * chip - 2 + h, 0)))
+                act(h, ts.at[2, h], jnp.maximum(2 * chip - 2 + h, 0))
 
             if h == 1:
                 @pl.when(chip == 2)
                 def _():
-                    act(half_copies(tm, h, ts.at[1, h], 7))
-
-    def start(copies):
-        for copy in copies:
-            copy.start()
-
-    def sent(copies):
-        for copy in copies:
-            copy.wait_send()
-
-    def landed(copies):
-        for copy in copies:
-            copy.wait_recv()
-
-    own_sends(start)
+                    act(h, ts.at[1, h], 7)
+
+    own_sends(lambda h, sem, target: start(half_copies(tm, h, sem, target)))
 
     def slab_at(e):
-        dx = jnp.where(e >= 5, 2, jnp.where(e % 2 == 1, 1, 3))
-        odd = jnp.where((e == 1) | (e == 2) | (e == 5), 1, 0)
+        dx = jnp.where((e == 1) | (e == 3), 1, jnp.where((e == 2) | (e == 5), 3, 2))
+        odd = jnp.where((e == 1) | (e == 2) | (e == 4), 1, 0)
         k = jnp.where(e == 0, 2 * chip + 1, 2 * (chip + dx) + odd)
         valid = (e == 0) | (chip + dx <= 3)
         return jnp.minimum(k, 7), dx, odd, valid
@@ -533,7 +535,7 @@
             @pl.when((e > 0) | (core == 0))
             def _():
                 with jax.named_scope("b1_slabwait"):
-                    landed(half_copies(k, core, ts.at[0, 0], sib))
+                    landed(k, core)
 
             @pl.when((dx == 1) & (core == 0) & ((chip == 1) | (chip == 2)) & (e > 0))
             def _():
@@ -563,7 +565,7 @@
         @pl.when(valid & (k > tm))
         def _():
             with jax.named_scope("b1_sibwait"):
-                landed(half_copies(k, 1 - core, ts.at[0, 0], sib))
+                landed(k, 1 - core)
             unpack(k, 1 - core)
             cross_sums(k, 1 - core)
 
@@ -591,7 +593,7 @@
     @pl.when(tm == 7)
     def _():
         for odd in (1, 0):
-            landed(half_copies(4 + odd, 1, ts.at[0, 0], sib))
+            landed(4 + odd, 1)
             start(half_copies(4 + odd, 1, rs.at[odd], 1))
 
     phase("b1_arrive")
@@ -606,64 +608,54 @@
     gram = jnp.sum(gram, axis=1)
     lane4 = lane_iota((8, 16, LANES))
     sub4 = lax.broadcasted_iota(jnp.int32, (8, 16, LANES), 1)
-    cross = jnp.where(lane4 == 64 + sub4, jnp.sum(CR[...], axis=2, keepdims=True), 0.0)
-    gram = gram + jnp.sum(cross, axis=1)
+    slab4 = lax.broadcasted_iota(jnp.int32, (8, 16, LANES), 0)
+    cross = jnp.where(
+        (lane4 == 13 * slab4 + sub4) & (sub4 < 13), jnp.sum(CR[...], axis=2, keepdims=True), 0.0
+    )
+    cross = jnp.sum(jnp.sum(cross, axis=0), axis=0, keepdims=True)
     lane5 = lane_iota((24, LANES))
     sub5 = lax.broadcasted_iota(jnp.int32, (24, LANES), 0)
-    own = jnp.where(lane5 == 80 + sub5, jnp.sum(KQ[...], axis=1, keepdims=True), 0.0)
-    own = jnp.sum(own, axis=0, keepdims=True)
-    gram = gram + jnp.where(lax.broadcasted_iota(jnp.int32, (8, LANES), 0) == 0, own, 0.0)
-    GM[...] = gram
-    GR[core * 16 + me] = gram
+    own = jnp.where(lane5 == 104 + sub5, jnp.sum(KQ[...], axis=1, keepdims=True), 0.0)
+    own = cross + jnp.sum(own, axis=0, keepdims=True)
+    sub2 = lax.broadcasted_iota(jnp.int32, (8, LANES), 0)
+    folded = jnp.where(lane2 < 64, pltpu.roll(gram, 4, 0), pltpu.roll(gram, 64, 1))
+    message = jnp.where(sub2 < 4, folded, jnp.where(sub2 == 4, own, 0.0))
+    GM[...] = message
+    GR[core * 16 + me] = message
     pl.semaphore_wait(plane_sem, 1)
-
-    def send_gram(step, _):
-        there = lax.rem(me + step, 16)
-        place = {"lat": there // 4, "lon": there % 4}
-
-        @pl.when(step < 16)
-        def _():
+    for a, b in far_first + [(0, 0)]:
+        targets = [{"tm": sib, **plane_peer(a, b)}] + ([plane_peer(a, b)] if (a, b) != (0, 0) else [])
+        for target in targets:
             pltpu.make_async_remote_copy(
-                GM, GR.at[core * 16 + me], gs, gr, device_id=place, device_id_type=MESH
+                GM.at[pl.ds(0, 5)], GR.at[core * 16 + me, pl.ds(0, 5)], gs, gr,
+                device_id=target, device_id_type=MESH,
             ).start()
-
-        pltpu.make_async_remote_copy(
-            GM, GR.at[core * 16 + me], gs, gr, device_id={"tm": sib, **place}, device_id_type=MESH
-        ).start()
-        return 0
-
-    lax.fori_loop(1, 17, send_gram, 0)
     phase("b3_wait")
-    box = GR.at[pl.ds(0, 31)]
-    pltpu.make_async_copy(box, box, gr).wait()
+    wait_rows(gr, 31 * 5)
     total = jnp.sum(GR[...], axis=0)
     plane = jnp.sum(GR[pl.ds(core * 16, 16)], axis=0)
     phase("b4_chain")
 
-    lane = lane_iota((8, LANES))
-
-    def column(source, i):
-        picked = jnp.sum(jnp.where(lane == i, source, 0.0), axis=1, keepdims=True)
-        return jnp.broadcast_to(picked, (8, LANES))
-
-    table = [[None if j == 0 else column(total, 8 * i + j) for j in range(8)] for i in range(8)]
-    with_g = [column(plane, 64 + i) for i in range(13)]
-    first_row = [column(plane, 80 + i)[0:1, :] for i in range(24)]
+    high_slabs = [diagonal(total[k : k + 1, :], LANES) for k in range(4)]
+    own_sums = diagonal(plane[4:5, :], LANES)
+    with_g = [[own_sums[13 * k + i : 13 * k + i + 1, :] for k in range(8)] for i in range(13)]
+    first_row = [own_sums[104 + i : 105 + i, :] for i in range(24)]
     k33, k32, k22 = first_row[:6], first_row[6:11], first_row[11:15]
 
     def entry(i, k, j):
-        return table[i][j][k : k + 1, :]
+        at = 8 * i + j if k >= 4 else 64 + 8 * i + j
+        return high_slabs[k % 4][at : at + 1, :]
 
     one = jnp.ones((1, LANES), jnp.float32)
     zero = jnp.zeros((1, LANES), jnp.float32)
     coefs = {7: one}
     quad = [entry(i, 7, 7) for i in range(8)]
     cross = [{j: entry(i, 7, j) for j in range(1, 7)} for i in range(8)]
-    mixed = [x[7:8, :] for x in with_g]
+    mixed = [x[7] for x in with_g]
     is_last = jnp.full((1, LANES), tm == 7)
     held_c = {k: zero for k in range(1, 8)}
     held_q = first_row[16:24]
-    held_m = [x[0:1, :] for x in with_g]
+    held_m = [x[0] for x in with_g]
     for t in range(7, 0, -1):
         if t < 7:
             psi_t = quad[0] / (quad[0] + 4.0 * quad[1] + EPS)
@@ -672,7 +664,7 @@
                 for i in range(8)
             ]
             cross = [{j: psi_t * cross[i][j] + entry(i, t, j) for j in range(1, t)} for i in range(8)]
-            mixed = [psi_t * x + y[t : t + 1, :] for x, y in zip(mixed, with_g)]
+            mixed = [psi_t * x + y[t] for x, y in zip(mixed, with_g)]
             coefs = {k: psi_t * x for k, x in coefs.items()}
             coefs[t] = one
         now = jnp.full((1, LANES), tm + 1 == t)
@@ -731,27 +723,22 @@
         put(0, row, scaled(psi, V[:4, part, :]) + TH[row // 80, tm, :4, first : first + count, :])
 
     phase("c9_end")
-    for copy in halos:
-        copy.wait_send()
+    wait_rows(hs, 4 * 8 + 2 * 48 + 4 * 96)
     for r in range(2):
-        box = AR.at[r, pl.ds(0, 15)]
-        pltpu.make_async_copy(box, box, ar_s.at[r]).wait()
-    box = GR.at[pl.ds(0, 31)]
-    pltpu.make_async_copy(box, box, gs).wait()
-    own_sends(sent)
+        wait_rows(ar_s.at[r], 15)
+    wait_rows(gs, 31 * 5)
+    own_sends(lambda h, sem, target: sent(sem))
     for e in range(1, 7):
-        k, _, _, valid = slab_at(e)
-
-        @pl.when(valid)
+        @pl.when(slab_at(e)[3])
         def _():
-            sent(half_copies(k, core, fs.at[e], sib))
+            sent(fs.at[e])
 
     relays = ((core == 0) & ((chip == 1) | (chip == 2))) | ((core == 1) & ((chip == 0) | (chip == 3)))
 
     @pl.when(relays)
     def _():
         for odd in range(2):
-            sent(half_copies(0, core, rs.at[odd], sib))
+            sent(rs.at[odd])
 
     phase(None)
 
@@ -792,20 +779,20 @@
             pltpu.VMEM((4, 8, LANES), f32),
             pltpu.VMEM((4, 8, LANES), f32),
             pltpu.VMEM((8, 2, 8, LANES), f32),
+            pltpu.VMEM((2, 8, LANES), f32),
             pltpu.VMEM((2, 16, LANES), f32),
-            pltpu.VMEM((2, 16, 16, LANES), f32),
             pltpu.VMEM((8, LANES), f32),
             pltpu.VMEM((32, 8, LANES), f32),
-            dma((7, 4)),
-            dma((10,)),
-            dma((10,)),
+            pltpu.VMEM((512, LANES), f32),
+            dma((3,)),
+            dma,
             dma((2,)),
             dma((2,)),
-            dma((3, 2, 2)),
+            dma((2,)),
+            dma((3, 2)),
             dma((8, 2)),
-            dma((8, 2)),
-            dma((7, 2)),
-            dma((2, 2)),
+            dma((7,)),
+            dma((2,)),
             dma,
             dma,
             pltpu.SemaphoreType.REGULAR,

time: 47.6 us -> 45.1 us (0.947)
  Pallas kernels: 46.4 us -> 44 us
    pallas_call x1, Pallas kernels: 46.4 us -> 44 us  [local(): pl.pallas_call(kernel, out_shape=jax.ShapeDtypeStruct(forcing.shape, f32)...]
where the time goes in v5:
time: 45.1 us; the launch traced here: 45 us
  Pallas kernels  44 us (98%)
  local copies, waits for them, and re-layouts  0.97 us (2%)
    pallas_call x1, Pallas kernels, local(): pl.pallas_call(kernel, out_shape=jax.ShapeDtypeStruct(forcing.shape, f32)...  44 us
    unnamed x1, local copies, waits for them, and re-layouts  0.97 us

profile of v5, /device:TPU:1, one launch (start us, length us, event | category | flops | bytes accessed | tf_op | source)
XLA Modules:
  0.0 45.0 jit_solution(15781440475624195361)
XLA Ops:
  0.0 44.0 %cycle.1 = f32[4,128,512]{2,1,0:T(8,128)S(1)} custom-call(f32[4,128,512]{2,1,0:T(8,128)} %forcing.1, f32[128,512]{1,0:T(8,128)} %depth.1, s32[128,512]{1,0:T(8,128)} %mask.1, f32[1,128,512]{2,1,0:T(8,128)} %guess.1), custom_call_target="tpu_custom_call" | custom-call | tf_op jit(solution)/shard_map/cycle/pallas_call | solution.py:751
  44.0 1.0 %copy.6 = f32[4,128,512]{2,1,0:T(8,128)} copy(f32[4,128,512]{2,1,0:T(8,128)S(1)} %cycle.1) | data formatting | bytes 2097152

commit v6 on v5

--- a/solution.py
+++ b/solution.py
@@ -135,10 +135,10 @@
         pltpu.make_async_copy(
             guess.at[0, :, cols(c)], F.at[CG, c, own_rows, :], in_sem.at[2]
         ).start()
-    for field, level in ((G3, 3), (G2, 2), (G1, 1), (G0, 0)):
+    for field, level, i in ((G3, 3, 2), (G2, 2, 3), (G1, 1, 3), (G0, 0, 3)):
         for c in range(4):
             pltpu.make_async_copy(
-                forcing.at[level, :, cols(c)], F.at[field, c, own_rows, :], in_sem.at[2]
+                forcing.at[level, :, cols(c)], F.at[field, c, own_rows, :], in_sem.at[i]
             ).start()
 
     phase("a1_clear")
@@ -168,32 +168,54 @@
         clear(LG.at[i])
 
     phase("a2_loadwait")
-    fields = F.at[pl.ds(1, 5), pl.ds(0, 4), own_rows, :]
+    fields = F.at[pl.ds(1, 2), pl.ds(0, 4), own_rows, :]
     for i, ref in enumerate((DEP, MSK, fields)):
         pltpu.make_async_copy(ref, ref, in_sem.at[i]).wait()
     for c in range(4):
         F[DM, c, LOW:END, :] = jnp.where(MSK[c] > 0, DEP[c], 0.0)
 
     phase("a3_pack")
-    lane6 = lane_iota((6, 8, LANES))
-    right_edge = jnp.zeros((6, 8, LANES), jnp.float32)
-    left_edge = jnp.zeros((6, 8, LANES), jnp.float32)
-    for t in range(16):
-        here = (lane6 >= 8 * t) & (lane6 < 8 * t + 8)
-        rows = slice(LOW + 8 * t, LOW + 8 * t + 8)
-        right_edge = jnp.where(here, pltpu.roll(F[:, 3, rows, :], (8 * t + 8) % LANES, 2), right_edge)
-        left_edge = jnp.where(here, pltpu.roll(F[:, 0, rows, :], 8 * t, 2), left_edge)
-    PKS[0] = right_edge
-    PKS[1] = left_edge
+    lane3f = lane_iota((3, 8, LANES))
     lane1 = lane_iota((8, LANES))
     corners = ((136, 3, 8), (136, 0, 0), (16, 3, 8), (16, 0, 0))
-    for i, (row, tile, shift) in enumerate(corners):
-        packed = jnp.zeros((8, LANES), jnp.float32)
-        for f in range(6):
-            here = (lane1 >= 8 * f) & (lane1 < 8 * f + 8)
-            edge = pltpu.roll(F[f, tile, row : row + 8, :], (8 * f + shift) % LANES, 1)
-            packed = jnp.where(here, edge, packed)
-        CKS[i] = packed
+
+    def pack(group):
+        three = slice(3 * group, 3 * group + 3)
+        right_edge = jnp.zeros((3, 8, LANES), jnp.float32)
+        left_edge = jnp.zeros((3, 8, LANES), jnp.float32)
+        for t in range(16):
+            here = (lane3f >= 8 * t) & (lane3f < 8 * t + 8)
+            rows = slice(LOW + 8 * t, LOW + 8 * t + 8)
+            right = pltpu.roll(F[three, 3, rows, :], (8 * t + 8) % LANES, 2)
+            right_edge = jnp.where(here, right, right_edge)
+            left_edge = jnp.where(here, pltpu.roll(F[three, 0, rows, :], 8 * t, 2), left_edge)
+        PKS[group, 0] = right_edge
+        PKS[group, 1] = left_edge
+        for i, (row, tile, shift) in enumerate(corners):
+            packed = jnp.zeros((8, LANES), jnp.float32)
+            for f in range(3):
+                here = (lane1 >= 8 * f) & (lane1 < 8 * f + 8)
+                edge = F[3 * group + f, tile, row : row + 8, :]
+                packed = jnp.where(here, pltpu.roll(edge, (8 * f + shift) % LANES, 1), packed)
+            CKS[group, i] = packed
+
+    def unpack_halo(group):
+        three = slice(3 * group, 3 * group + 3)
+        from_left, from_right = PKR[group, 0], PKR[group, 1]
+        for t in range(16):
+            rows = slice(LOW + 8 * t, LOW + 8 * t + 8)
+            a = pltpu.roll(from_left, (120 - 8 * t) % LANES, 2)
+            b = pltpu.roll(from_right, (LANES - 8 * t) % LANES, 2)
+            F[three, 4, rows, :] = jnp.where(lane3f >= 120, a, jnp.where(lane3f < 8, b, 0.0))
+        for row, left, right in ((8, 0, 1), (144, 2, 3)):
+            a0, b0 = CKR[group, left], CKR[group, right]
+            for f in range(3):
+                a = pltpu.roll(a0, (120 - 8 * f) % LANES, 1)
+                b = pltpu.roll(b0, (LANES - 8 * f) % LANES, 1)
+                edge = jnp.where(lane1 >= 120, a, jnp.where(lane1 < 8, b, 0.0))
+                F[3 * group + f, 4, row : row + 8, :] = edge
+
+    pack(0)
 
     phase("a4_barrier")
     pl.semaphore_wait(barrier, 15)
@@ -209,39 +231,36 @@
         pltpu.make_async_copy(box, box, sem).wait()
 
     targets = ((south, east), (south, west), (north, east), (north, west))
-    for i, (a, b) in enumerate(targets):
-        push(CKS.at[i], CKR.at[i], 0, {"lat": a, "lon": b})
-    push(PKS.at[0], PKR.at[0], 0, {"lon": east})
-    push(PKS.at[1], PKR.at[1], 0, {"lon": west})
-    for i, first in ((0, 0), (1, 3)):
-        group = pl.ds(first, 3)
+
+    def push_halo(group):
+        for i, (a, b) in enumerate(targets):
+            push(CKS.at[group, i], CKR.at[group, i], group, {"lat": a, "lon": b})
+        fields = pl.ds(3 * group, 3)
         push(
-            F.at[group, pl.ds(0, 4), pl.ds(136, 8), :],
-            F.at[group, pl.ds(0, 4), pl.ds(8, 8), :],
-            i, {"lat": south},
+            F.at[fields, pl.ds(0, 4), pl.ds(136, 8), :],
+            F.at[fields, pl.ds(0, 4), pl.ds(8, 8), :],
+            group, {"lat": south},
         )
         push(
-            F.at[group, pl.ds(0, 4), pl.ds(16, 8), :],
-            F.at[group, pl.ds(0, 4), pl.ds(144, 8), :],
-            i, {"lat": north},
+            F.at[fields, pl.ds(0, 4), pl.ds(16, 8), :],
+            F.at[fields, pl.ds(0, 4), pl.ds(144, 8), :],
+            group, {"lat": north},
         )
+        push(PKS.at[group, 0], PKR.at[group, 0], group, {"lon": east})
+        push(PKS.at[group, 1], PKR.at[group, 1], group, {"lon": west})
+
+    halo_rows = 4 * 8 + 2 * 96 + 2 * 24
+    push_halo(0)
+    fields = F.at[pl.ds(3, 3), pl.ds(0, 4), own_rows, :]
+    pltpu.make_async_copy(fields, fields, in_sem.at[3]).wait()
+    pack(1)
+    push_halo(1)
     phase("a5_halowait")
-    wait_rows(hr.at[0], 4 * 8 + 2 * 48 + 2 * 96)
+    wait_rows(hr.at[0], halo_rows)
 
     pl.semaphore_signal(plane_sem, inc=1, device_id={"tm": sib}, device_id_type=MESH)
     phase("a6_unpack")
-    from_left, from_right = PKR[0], PKR[1]
-    for t in range(16):
-        rows = slice(LOW + 8 * t, LOW + 8 * t + 8)
-        a = pltpu.roll(from_left, (120 - 8 * t) % LANES, 2)
-        b = pltpu.roll(from_right, (LANES - 8 * t) % LANES, 2)
-        F[:, 4, rows, :] = jnp.where(lane6 >= 120, a, jnp.where(lane6 < 8, b, 0.0))
-    for row, left, right in ((8, 0, 1), (144, 2, 3)):
-        a0, b0 = CKR[left], CKR[right]
-        for f in range(6):
-            a = pltpu.roll(a0, (120 - 8 * f) % LANES, 1)
-            b = pltpu.roll(b0, (LANES - 8 * f) % LANES, 1)
-            F[f, 4, row : row + 8, :] = jnp.where(lane1 >= 120, a, jnp.where(lane1 < 8, b, 0.0))
+    unpack_halo(0)
 
     inside_top = jnp.where(lat > 0, 1.0, 0.0).astype(jnp.float32)
     inside_end = jnp.where(lat < 3, 1.0, 0.0).astype(jnp.float32)
@@ -389,7 +408,8 @@
     prepare(G3, 0)
 
     def rest_of_halo():
-        wait_rows(hr.at[1], 2 * 96)
+        wait_rows(hr.at[1], halo_rows)
+        unpack_halo(1)
         prepare(G1, 1)
         powers_of_g3()
         rows = pl.ds(pl.multiple_of(8 + 64 * core, 8), 80)
@@ -483,6 +503,16 @@
             back = jnp.where((lane2 < 4) | (lane2 >= 124), back, 0.0)
             TH[h, k, 4, 8 + 8 * t : 16 + 8 * t, :] = back
 
+    def cross_sums(k, h):
+        sums = Sums()
+        rows = pl.ds(pl.multiple_of(HALF_LOW + 64 * h, 8), HALF_END - HALF_LOW)
+        for t in range(4):
+            value = TH[h, k, t, HALF_LOW:HALF_END, :]
+            for i, ref in enumerate(g3_powers + g2_powers):
+                sums.add(i, value, ref[t, rows, :])
+        for i in range(13):
+            CR[k, i : i + 1, :] = CR[k, i : i + 1, :] + line(sums.terms[i])
+
     def gram_sums(e, k):
         refs = [TH.at[core, k], UG.at[k], TG2.at[k], TG3.at[k]]
         for src, dst in zip(refs, refs[1:]):
@@ -491,6 +521,7 @@
         for row, count in HALF_OWN:
             last_power = spread(refs[3], KH, row, count)[1]
             TG4[k, :, row - HALF_LOW : row - HALF_LOW + count, :] = last_power[:4]
+        cross_sums(k, core)
 
         def pair(q, _):
             j, _, _, held = slab_at(q)
@@ -517,16 +548,6 @@
 
         lax.fori_loop(0, e + 1, pair, 0)
 
-    def cross_sums(k, h):
-        sums = Sums()
-        rows = pl.ds(pl.multiple_of(HALF_LOW + 64 * h, 8), HALF_END - HALF_LOW)
-        for t in range(4):
-            value = TH[h, k, t, HALF_LOW:HALF_END, :]
-            for i, ref in enumerate(g3_powers + g2_powers):
-                sums.add(i, value, ref[t, rows, :])
-        for i in range(13):
-            CR[k, i : i + 1, :] = CR[k, i : i + 1, :] + line(sums.terms[i])
-
     def first_hand(e):
         k, dx, odd, valid = slab_at(e)
 
@@ -549,15 +570,8 @@
             def _():
                 start(half_copies(k, core, fs.at[e], sib))
 
-            @pl.when(k > tm)
-            def _():
-                unpack(k, core)
-
+            unpack(k, core)
             gram_sums(e, k)
-
-            @pl.when(k > tm)
-            def _():
-                cross_sums(k, core)
 
     def second_hand(e):
         k, _, _, valid = slab_at(e)
@@ -574,9 +588,9 @@
         def _():
             first_hand(jnp.minimum(i, 6))
 
-        @pl.when(i >= 3)
+        @pl.when(i >= 2)
         def _():
-            second_hand(jnp.maximum(i - 3, 0))
+            second_hand(jnp.maximum(i - 2, 0))
 
         return 0
 
@@ -597,7 +611,7 @@
             start(half_copies(4 + odd, 1, rs.at[odd], 1))
 
     phase("b1_arrive")
-    lax.fori_loop(0, 10, arrive, 0)
+    lax.fori_loop(0, 9, arrive, 0)
 
     phase("b2_gram")
     lane3 = lane_iota((8, 8, LANES))
@@ -723,7 +737,7 @@
         put(0, row, scaled(psi, V[:4, part, :]) + TH[row // 80, tm, :4, first : first + count, :])
 
     phase("c9_end")
-    wait_rows(hs, 4 * 8 + 2 * 48 + 4 * 96)
+    wait_rows(hs, 2 * halo_rows)
     for r in range(2):
         wait_rows(ar_s.at[r], 15)
     wait_rows(gs, 31 * 5)
@@ -774,17 +788,17 @@
             pltpu.VMEM((8, 8, 8, LANES), f32),
             pltpu.VMEM((8, 16, LANES), f32),
             pltpu.VMEM((24, LANES), f32),
-            pltpu.VMEM((2, 6, 8, LANES), f32),
-            pltpu.VMEM((2, 6, 8, LANES), f32),
-            pltpu.VMEM((4, 8, LANES), f32),
-            pltpu.VMEM((4, 8, LANES), f32),
+            pltpu.VMEM((2, 2, 3, 8, LANES), f32),
+            pltpu.VMEM((2, 2, 3, 8, LANES), f32),
+            pltpu.VMEM((2, 4, 8, LANES), f32),
+            pltpu.VMEM((2, 4, 8, LANES), f32),
             pltpu.VMEM((8, 2, 8, LANES), f32),
             pltpu.VMEM((2, 8, LANES), f32),
             pltpu.VMEM((2, 16, LANES), f32),
             pltpu.VMEM((8, LANES), f32),
             pltpu.VMEM((32, 8, LANES), f32),
-            pltpu.VMEM((512, LANES), f32),
-            dma((3,)),
+            pltpu.VMEM((544, LANES), f32),
+            dma((4,)),
             dma,
             dma((2,)),
             dma((2,)),

time: 45.1 us -> 44.7 us (level)
  Pallas kernels: 44 us -> 43.5 us
    pallas_call x1, Pallas kernels: 44 us -> 43.5 us  [local(): pl.pallas_call(kernel, out_shape=jax.ShapeDtypeStruct(forcing.shape, f32)...]
where the time goes in v6:
time: 44.7 us; the launch traced here: 44.5 us
  Pallas kernels  43.5 us (97%)
  local copies, waits for them, and re-layouts  0.97 us (2%)
    pallas_call x1, Pallas kernels, local(): pl.pallas_call(kernel, out_shape=jax.ShapeDtypeStruct(forcing.shape, f32)...  43.5 us
    unnamed x1, local copies, waits for them, and re-layouts  0.97 us

profile of v6, /device:TPU:1, one launch (start us, length us, event | category | flops | bytes accessed | tf_op | source)
XLA Modules:
  0.0 44.5 jit_solution(1532967961425654266)
XLA Ops:
  0.0 43.5 %cycle.1 = f32[4,128,512]{2,1,0:T(8,128)S(1)} custom-call(f32[4,128,512]{2,1,0:T(8,128)} %forcing.1, f32[128,512]{1,0:T(8,128)} %depth.1, s32[128,512]{1,0:T(8,128)} %mask.1, f32[1,128,512]{2,1,0:T(8,128)} %guess.1), custom_call_target="tpu_custom_call" | custom-call | tf_op jit(solution)/shard_map/cycle/pallas_call | solution.py:765
  43.5 1.0 %copy.6 = f32[4,128,512]{2,1,0:T(8,128)} copy(f32[4,128,512]{2,1,0:T(8,128)S(1)} %cycle.1) | data formatting | bytes 2097152

commit v7 on v6

--- a/solution.py
+++ b/solution.py
@@ -530,19 +530,17 @@
             def _():
                 sums = Sums()
                 low, high = jnp.minimum(j, k), jnp.maximum(j, k)
-                for t in range(4):
+                for t, (row, count) in ((t, rows) for t in range(4) for rows in HALF_OWN):
+                    part = slice(row, row + count)
                     a, b = (
-                        [TH[core, s, t, HALF_LOW:HALF_END, :]]
-                        + [ref[s, t, HALF_LOW:HALF_END, :] for ref in (UG, TG2, TG3)]
+                        [TH[core, s, t, part, :]] + [ref[s, t, part, :] for ref in (UG, TG2, TG3)]
                         for s in (low, high)
                     )
-                    b.append(TG4[high, t])
+                    b.append(TG4[high, t, row - HALF_LOW : row - HALF_LOW + count, :])
                     for i in range(8):
                         sums.add(i, a[i // 2], b[(i + 1) // 2])
                 for i in range(8):
-                    value = line(sums.terms[i])
-                    ROW[i, k, pl.ds(j, 1), :] = value
-                    ROW[i, j, pl.ds(k, 1), :] = value
+                    ROW[i, high, pl.ds(low, 1), :] = line(sums.terms[i])
 
             return 0
 
@@ -588,9 +586,9 @@
         def _():
             first_hand(jnp.minimum(i, 6))
 
-        @pl.when(i >= 2)
+        @pl.when(i >= 1)
         def _():
-            second_hand(jnp.maximum(i - 2, 0))
+            second_hand(jnp.maximum(i - 1, 0))
 
         return 0
 
@@ -611,7 +609,7 @@
             start(half_copies(4 + odd, 1, rs.at[odd], 1))
 
     phase("b1_arrive")
-    lax.fori_loop(0, 9, arrive, 0)
+    lax.fori_loop(0, 8, arrive, 0)
 
     phase("b2_gram")
     lane3 = lane_iota((8, 8, LANES))

time: 44.7 us -> 44.4 us (level)
  no operation moved by 1% of the time
where the time goes in v7:
time: 44.4 us; the launch traced here: 44.2 us
  Pallas kernels  43.3 us (98%)
  local copies, waits for them, and re-layouts  0.97 us (2%)
    pallas_call x1, Pallas kernels, local(): pl.pallas_call(kernel, out_shape=jax.ShapeDtypeStruct(forcing.shape, f32)...  43.3 us
    unnamed x1, local copies, waits for them, and re-layouts  0.97 us

profile of v7, /device:TPU:1, one launch (start us, length us, event | category | flops | bytes accessed | tf_op | source)
XLA Modules:
  0.0 44.2 jit_solution(11117475030559315971)
XLA Ops:
  0.0 43.3 %cycle.1 = f32[4,128,512]{2,1,0:T(8,128)S(1)} custom-call(f32[4,128,512]{2,1,0:T(8,128)} %forcing.1, f32[128,512]{1,0:T(8,128)} %depth.1, s32[128,512]{1,0:T(8,128)} %mask.1, f32[1,128,512]{2,1,0:T(8,128)} %guess.1), custom_call_target="tpu_custom_call" | custom-call | tf_op jit(solution)/shard_map/cycle/pallas_call | solution.py:763
  43.3 1.0 %copy.6 = f32[4,128,512]{2,1,0:T(8,128)} copy(f32[4,128,512]{2,1,0:T(8,128)S(1)} %cycle.1) | data formatting | bytes 2097152

commit v8 on v7

--- a/solution.py
+++ b/solution.py
@@ -96,7 +96,7 @@
     forcing, depth, mask, guess, out,
     F, K, V, X, U, W, LG, GP, KH, TH, UG, TG2, TG3, TG4, DEP, MSK, KAP, ROW, CR, KQ,
     PKS, PKR, CKS, CKR, PT, MSG, AR,
-    GM, GR, BOX, in_sem, hs, hr, ar_s, ar_r, ts, tr, fs, rs, gs, gr, plane_sem,
+    GM, GR, BOX, in_sem, done, hr, ar_r, tr, gr, plane_sem,
 ):
     phase = Phase()
     phase("a0_load")
@@ -223,7 +223,7 @@
 
     def push(src, dst, i, target):
         pltpu.make_async_remote_copy(
-            src, dst, hs, hr.at[i], device_id=target, device_id_type=MESH
+            src, dst, done, hr.at[i], device_id=target, device_id_type=MESH
         ).start()
 
     def wait_rows(sem, count):
@@ -300,7 +300,7 @@
         AR[r, pl.ds(me, 1), :] = message
         for a, b in far_first:
             pltpu.make_async_remote_copy(
-                MSG.at[r, pl.ds(0, 1)], AR.at[r, pl.ds(me, 1)], ar_s.at[r], ar_r.at[r],
+                MSG.at[r, pl.ds(0, 1)], AR.at[r, pl.ds(me, 1)], done, ar_r.at[r],
                 device_id=plane_peer(a, b), device_id_type=MESH,
             ).start()
 
@@ -462,9 +462,6 @@
         for copy in copies:
             copy.start()
 
-    def sent(sem):
-        wait_rows(sem, 4 * 72 + 8)
-
     def landed(k, h):
         wait_rows(tr.at[k, h], 4 * 72 + 8)
 
@@ -472,20 +469,20 @@
         for h in range(2):
             @pl.when(core == 1)
             def _():
-                act(h, ts.at[0, h], sib)
+                act(h, done, sib)
 
             @pl.when(chip == 3)
             def _():
-                act(h, ts.at[1, h], h)
+                act(h, done, h)
 
             @pl.when(chip >= 1)
             def _():
-                act(h, ts.at[2, h], jnp.maximum(2 * chip - 2 + h, 0))
+                act(h, done, jnp.maximum(2 * chip - 2 + h, 0))
 
             if h == 1:
                 @pl.when(chip == 2)
                 def _():
-                    act(h, ts.at[1, h], 7)
+                    act(h, done, 7)
 
     own_sends(lambda h, sem, target: start(half_copies(tm, h, sem, target)))
 
@@ -558,15 +555,15 @@
 
             @pl.when((dx == 1) & (core == 0) & ((chip == 1) | (chip == 2)) & (e > 0))
             def _():
-                start(half_copies(k, 0, rs.at[odd], jnp.maximum(tm - 2, 0)))
+                start(half_copies(k, 0, done, jnp.maximum(tm - 2, 0)))
 
             @pl.when((dx == 3) & (core == 1) & (chip == 0) & (e > 0))
             def _():
-                start(half_copies(k, 1, rs.at[odd], 3))
+                start(half_copies(k, 1, done, 3))
 
             @pl.when(e > 0)
             def _():
-                start(half_copies(k, core, fs.at[e], sib))
+                start(half_copies(k, core, done, sib))
 
             unpack(k, core)
             gram_sums(e, k)
@@ -606,7 +603,7 @@
     def _():
         for odd in (1, 0):
             landed(4 + odd, 1)
-            start(half_copies(4 + odd, 1, rs.at[odd], 1))
+            start(half_copies(4 + odd, 1, done, 1))
 
     phase("b1_arrive")
     lax.fori_loop(0, 8, arrive, 0)
@@ -639,7 +636,7 @@
         targets = [{"tm": sib, **plane_peer(a, b)}] + ([plane_peer(a, b)] if (a, b) != (0, 0) else [])
         for target in targets:
             pltpu.make_async_remote_copy(
-                GM.at[pl.ds(0, 5)], GR.at[core * 16 + me, pl.ds(0, 5)], gs, gr,
+                GM.at[pl.ds(0, 5)], GR.at[core * 16 + me, pl.ds(0, 5)], done, gr,
                 device_id=target, device_id_type=MESH,
             ).start()
     phase("b3_wait")
@@ -735,22 +732,11 @@
         put(0, row, scaled(psi, V[:4, part, :]) + TH[row // 80, tm, :4, first : first + count, :])
 
     phase("c9_end")
-    wait_rows(hs, 2 * halo_rows)
-    for r in range(2):
-        wait_rows(ar_s.at[r], 15)
-    wait_rows(gs, 31 * 5)
-    own_sends(lambda h, sem, target: sent(sem))
-    for e in range(1, 7):
-        @pl.when(slab_at(e)[3])
+    fixed = 2 * halo_rows + 2 * 15 + 31 * 5
+    for place, halves in enumerate((6, 10, 8, 8, 7, 7, 4, 8)):
+        @pl.when(tm == place)
         def _():
-            sent(fs.at[e])
-
-    relays = ((core == 0) & ((chip == 1) | (chip == 2))) | ((core == 1) & ((chip == 0) | (chip == 3)))
-
-    @pl.when(relays)
-    def _():
-        for odd in range(2):
-            sent(rs.at[odd])
+            wait_rows(done, fixed + halves * (4 * 72 + 8))
 
     phase(None)
 
@@ -795,17 +781,12 @@
             pltpu.VMEM((2, 16, LANES), f32),
             pltpu.VMEM((8, LANES), f32),
             pltpu.VMEM((32, 8, LANES), f32),
-            pltpu.VMEM((544, LANES), f32),
+            pltpu.VMEM((3696, LANES), f32),
             dma((4,)),
             dma,
             dma((2,)),
             dma((2,)),
-            dma((2,)),
-            dma((3, 2)),
             dma((8, 2)),
-            dma((7,)),
-            dma((2,)),
-            dma,
             dma,
             pltpu.SemaphoreType.REGULAR,
         ],

time: 44.4 us -> 44.2 us (level)
  no operation moved by 1% of the time
where the time goes in v8:
time: 44.2 us; the launch traced here: 44.1 us
  Pallas kernels  43.1 us (98%)
  local copies, waits for them, and re-layouts  0.97 us (2%)
    pallas_call x1, Pallas kernels, local(): pl.pallas_call(kernel, out_shape=jax.ShapeDtypeStruct(forcing.shape, f32)...  43.1 us
    unnamed x1, local copies, waits for them, and re-layouts  0.97 us

profile of v8, /device:TPU:1, one launch (start us, length us, event | category | flops | bytes accessed | tf_op | source)
XLA Modules:
  0.0 44.1 jit_solution(8952316509139364859)
XLA Ops:
  0.0 43.1 %cycle.1 = f32[4,128,512]{2,1,0:T(8,128)S(1)} custom-call(f32[4,128,512]{2,1,0:T(8,128)} %forcing.1, f32[128,512]{1,0:T(8,128)} %depth.1, s32[128,512]{1,0:T(8,128)} %mask.1, f32[1,128,512]{2,1,0:T(8,128)} %guess.1), custom_call_target="tpu_custom_call" | custom-call | tf_op jit(solution)/shard_map/cycle/pallas_call | solution.py:749
  43.1 1.0 %copy.6 = f32[4,128,512]{2,1,0:T(8,128)} copy(f32[4,128,512]{2,1,0:T(8,128)S(1)} %cycle.1) | data formatting | bytes 2097152
